TPU v7x, 32 devices: a whole 2x2x4 slice. The times are simulated.
32 devices in a mesh: patch: 4 (over z), seq: 4 (over y, x), req: 2 (over core).
Axes of the slice: x: 2, y: 2, z: 4, core: 2. Of those that a mesh axis runs over, the one named last changes fastest.
Arguments:
- query: bfloat16 [4, 8, 3584], P(None, ('patch', 'req')), may hold values from -20 to 20
- text_cache: bfloat16 [4, 8, 3072, 1024], P(None, ('patch', 'req'), 'seq'), may hold values from -6 to 6
- text_len: int32 [8], P(('patch', 'req')), may hold values from 0 to 3072
- image_rows: bfloat16 [4, 8192, 1024], P(None, ('patch', 'seq', 'req')), may hold values from -6 to 6
- patch_map: int32 [8192], P(('patch', 'seq', 'req')), may hold values from 0 to 7, as said below
- image_places: int32 [8192], P(('patch', 'seq', 'req')), may hold values from 0 to 1023, as said below
Outputs:
- attended: bfloat16 [4, 8, 3584], P(None, ('patch', 'req'), 'seq')
- image_cache: bfloat16 [4, 8, 1024, 1024], P(None, ('patch', 'req'), 'seq')
Inputs may be any that keep to these rules, and one draw needn't show every extreme that they name: `patch_map`: each aligned block of 256 rows (the rows of one prefill device) holds exactly 32 rows of every request. `image_places`: together with patch_map every pair of request and position occurs exactly once. The rows of a device whose seq index is s have positions from s * 256 to (s + 1) * 256 - 1.
All inputs are finite; a program needn't handle non-finite values.
Results may differ from a plain program's by a relative error of at most 0.0026.
Values may be sent and summed in bfloat16 or wider, within the bound.
A program may use at most 64 MiB of HBM per device.

v0:
```python
import functools
import math

import jax
import jax.numpy as jnp
from jax import lax
from jax.experimental import pallas as pl
from jax.experimental.pallas import tpu as pltpu
from jax.sharding import PartitionSpec as P

HEADS = 28
KV_HEADS = 4
HEAD_DIM = 128
PAD = 8
MESH = pl.DeviceIdType.MESH
NT = (((1,), (1,)), ((), ()))


def hop_order(patch_count, req_count):
    steps = sorted(range(1, patch_count), key=lambda d: -min(d, patch_count - d))
    pairs = [(d, c) for d in steps for c in range(req_count)]
    return pairs + [(0, c) for c in range(1, req_count)]


def kernel(
    dims,
    query_ref, len_hbm, map_hbm, place_hbm, rows_hbm, text_hbm,
    att_ref, cache,
    query, length, maps, places, rows, text, main_out, main_in, own_out, own_in, place_out, place_in,
    scores, image_ws, text_sums, image_sums, part_out, part_in,
    small_sem, rows_sem, text_sem, main_send, main_recv, own_send, own_recv,
    place_send, place_recv, part_send, part_recv,
):
    patch_count, seq_count, req_count = dims
    layers, src_rows, full = rows.shape
    text_dev = text.shape[1]
    kvw = full // 2
    group = HEADS // KV_HEADS
    groups = patch_count * req_count
    per = src_rows // groups
    main_width = full - HEAD_DIM
    scale = 1.0 / math.sqrt(HEAD_DIM)
    patch, seq, req = (lax.axis_index(a) for a in ("patch", "seq", "req"))
    me = patch * req_count + req
    hops = hop_order(patch_count, req_count)
    f32, bf16 = jnp.float32, jnp.bfloat16

    def partner(hop):
        p = lax.rem(patch + hop[0], patch_count)
        r = lax.rem(req + hop[1], req_count)
        return p, r

    barrier = pltpu.get_barrier_semaphore()
    for hop in hops:
        p, r = partner(hop)
        pl.semaphore_signal(barrier, inc=1, device_id=(p, seq, r), device_id_type=MESH)
    for d in range(1, seq_count):
        s = lax.rem(seq + d, seq_count)
        pl.semaphore_signal(barrier, inc=1, device_id=(patch, s, req), device_id_type=MESH)

    small = [
        pltpu.make_async_copy(map_hbm, maps, small_sem.at[0]),
        pltpu.make_async_copy(place_hbm, places, small_sem.at[1]),
        pltpu.make_async_copy(query_ref, query, small_sem.at[2]),
        pltpu.make_async_copy(len_hbm, length, small_sem.at[3]),
    ]
    for copy in small:
        copy.start()

    def rows_copy(l):
        return pltpu.make_async_copy(rows_hbm.at[l], rows.at[l], rows_sem.at[l])

    def text_copy(l):
        return pltpu.make_async_copy(text_hbm.at[l, 0], text.at[l], text_sem.at[l])

    rows_copy(0).start()

    def lanes_of(d):
        g = lax.rem(seq + d, seq_count)
        return pl.ds(pl.multiple_of(kvw + g * HEAD_DIM, HEAD_DIM), HEAD_DIM)

    owner = lax.broadcasted_iota(jnp.int32, (groups, src_rows), 0)
    row_i = lax.broadcasted_iota(jnp.int32, (src_rows, src_rows), 0)
    col_i = lax.broadcasted_iota(jnp.int32, (src_rows, src_rows), 1)
    before = (row_i < col_i).astype(f32).astype(bf16)
    small[0].wait()
    mine = maps[...] == owner
    rank = jnp.dot(mine.astype(f32).astype(bf16), before, preferred_element_type=f32)
    slot = jnp.sum(
        jnp.where(mine, rank + (owner * per).astype(f32), 0.0), axis=0, keepdims=True
    )
    pick = (row_i == slot.astype(jnp.int32)).astype(f32).astype(bf16)

    def place_copy(k, hop):
        p, r = partner(hop)
        return pltpu.make_async_remote_copy(
            src_ref=place_out, dst_ref=place_in.at[me],
            send_sem=place_send.at[k], recv_sem=place_recv.at[k],
            device_id=(p, seq, r), device_id_type=MESH,
        )

    def main_copy(l, k, hop):
        p, r = partner(hop)
        return pltpu.make_async_remote_copy(
            src_ref=main_out.at[l, p * req_count + r], dst_ref=main_in.at[l, me],
            send_sem=main_send.at[l, k], recv_sem=main_recv.at[l, k],
            device_id=(p, seq, r), device_id_type=MESH,
        )

    def own_copy(k, hop):
        p, r = partner(hop)
        return pltpu.make_async_remote_copy(
            src_ref=own_out.at[p * req_count + r], dst_ref=own_in.at[me],
            send_sem=own_send.at[k], recv_sem=own_recv.at[k],
            device_id=(p, seq, r), device_id_type=MESH,
        )

    def part_copy(l, d):
        s = lax.rem(seq + d, seq_count)
        return pltpu.make_async_remote_copy(
            src_ref=part_out.at[l, d], dst_ref=part_in.at[l, d],
            send_sem=part_send.at[l, d], recv_sem=part_recv.at[l, d],
            device_id=(patch, s, req), device_id_type=MESH,
        )

    for l in range(layers):
        rows_copy(l).wait()
        if l == 0:
            for m in range(1, layers):
                rows_copy(m).start()
        keys = jnp.dot(pick, rows[l, :, :kvw], preferred_element_type=f32).astype(bf16)
        main_out[l, :, :, :kvw] = keys.reshape(groups, per, kvw)
        others = jnp.concatenate(
            [rows[l, :, lanes_of(d)] for d in range(1, seq_count)] + [rows[l, :, lanes_of(0)]],
            axis=1,
        )
        moved = jnp.dot(pick, others, preferred_element_type=f32).astype(bf16)
        cut = main_width - kvw
        main_out[l, :, :, kvw:] = moved[:, :cut].reshape(groups, per, cut)
        own_out[:, l] = moved[:, cut:].reshape(groups, per, HEAD_DIM)
        if l == 0:
            pl.semaphore_wait(barrier, len(hops) + seq_count - 1)
        for k, hop in enumerate(hops):
            main_copy(l, k, hop).start()
        if l == 0:
            small[1].wait()
            local = (places[...] - seq * src_rows).astype(f32).astype(bf16)
            place_sorted = lax.dot_general(
                jnp.broadcast_to(local, (PAD, src_rows)), pick, NT,
                preferred_element_type=f32,
            )
            place_out[...] = place_sorted[0:1].astype(jnp.int32)
            place_in[me] = place_sorted[0:1].astype(jnp.int32)
            for k, hop in enumerate(hops):
                place_copy(k, hop).start()
    for k, hop in enumerate(hops):
        own_copy(k, hop).start()
    for l in range(layers):
        text_copy(l).start()
    for l in range(layers):
        main_in[l, me] = main_out[l, me]
    own_in[me] = own_out[me]

    positions = seq * text_dev + lax.broadcasted_iota(
        jnp.int32, (KV_HEADS * PAD, text_dev), 1
    )
    small[3].wait()
    used = positions < length[0:1, 0:1]
    zeros = jnp.zeros((PAD, HEAD_DIM), bf16)
    small[2].wait()
    lines = query[...].astype(f32)
    spread = []
    for l in range(layers):
        blocks = []
        for g in range(KV_HEADS):
            heads = [
                lines[l:l + 1, (g * group + h) * HEAD_DIM:(g * group + h + 1) * HEAD_DIM]
                for h in range(group)
            ] + [jnp.zeros((PAD - group, HEAD_DIM), f32)]
            block = jnp.concatenate(heads, axis=0).astype(bf16)
            blocks.append(
                jnp.concatenate(
                    [block if c == g else zeros for c in range(KV_HEADS)], axis=1
                )
            )
        spread.append(jnp.concatenate(blocks, axis=0))
    for l in range(layers):
        text_copy(l).wait()
        raw = lax.dot_general(
            spread[l], text[l, :, :kvw], NT, preferred_element_type=f32
        ) * scale
        scores[l] = jnp.where(used, raw, -jnp.inf)

    for k, hop in enumerate(hops):
        place_copy(k, hop).wait_recv()
    wanted = (row_i == me * per + lax.rem(col_i, per)).astype(f32).astype(bf16)
    lanes = jnp.dot(
        place_in[...].reshape(groups, src_rows).astype(f32).astype(bf16), wanted,
        preferred_element_type=f32,
    )
    source = lax.broadcasted_iota(jnp.int32, (groups, src_rows), 1) // per
    place = jnp.sum(jnp.where(source == owner, lanes, 0.0), axis=0, keepdims=True)
    put = (row_i == place.astype(jnp.int32)).astype(f32).astype(bf16)

    for l in range(layers):
        for k, hop in enumerate(hops):
            main_copy(l, k, hop).wait_recv()
        block = main_in[l].reshape(src_rows, main_width)
        image_scores = lax.dot_general(
            spread[l], block[:, :kvw], NT, preferred_element_type=f32
        ) * scale
        text_scores = scores[l]
        top = jnp.maximum(
            jnp.max(text_scores, axis=1, keepdims=True),
            jnp.max(image_scores, axis=1, keepdims=True),
        )
        text_w = jnp.exp(text_scores - top)
        image_w = jnp.exp(image_scores - top)
        total = jnp.sum(text_w, axis=1, keepdims=True) + jnp.sum(
            image_w, axis=1, keepdims=True
        )
        text_sums[:, :kvw] = jnp.dot(
            text_w.astype(bf16), text[l, :, kvw:], preferred_element_type=f32
        )
        text_sums[:, kvw:kvw + HEAD_DIM] = jnp.broadcast_to(top, (KV_HEADS * PAD, HEAD_DIM))
        text_sums[:, kvw + HEAD_DIM:] = jnp.broadcast_to(total, (KV_HEADS * PAD, HEAD_DIM))
        image_sums[...] = jnp.dot(
            image_w.astype(bf16), block[:, kvw:], preferred_element_type=f32
        )
        image_ws[l] = image_w
        for d in range(seq_count):
            g = lax.rem(seq + d, seq_count)
            at = pl.ds(pl.multiple_of(g * PAD, PAD), PAD)
            value = text_sums[at, pl.ds(pl.multiple_of(g * HEAD_DIM, HEAD_DIM), HEAD_DIM)]
            if d:
                value = value + image_sums[at, (d - 1) * HEAD_DIM:d * HEAD_DIM]
            part_out[l, d, :, :HEAD_DIM] = value
            part_out[l, d, :, HEAD_DIM:] = text_sums[at, kvw:]
            if d:
                part_copy(l, d).start()
        moved = jnp.dot(put, block, preferred_element_type=f32).astype(bf16)
        cache[l, 0, :, :kvw] = moved[:, :kvw]
        for d in range(1, seq_count):
            cache[l, 0, :, lanes_of(d)] = moved[
                :, kvw + (d - 1) * HEAD_DIM:kvw + d * HEAD_DIM
            ]

    partial = []
    for l in range(layers):
        for d in range(1, seq_count):
            part_copy(l, d).wait_recv()
        cells = [part_out[l, 0]] + [part_in[l, d] for d in range(1, seq_count)]
        tops = [c[:, HEAD_DIM:2 * HEAD_DIM] for c in cells]
        top = functools.reduce(jnp.maximum, tops)
        factors = [jnp.exp(t - top) for t in tops]
        total = sum(f * c[:, 2 * HEAD_DIM:] for f, c in zip(factors, cells))
        summed = sum(f * c[:, :HEAD_DIM] for f, c in zip(factors, cells))
        partial.append((factors[0], summed, total))

    for k, hop in enumerate(hops):
        own_copy(k, hop).wait_recv()
    at = pl.ds(pl.multiple_of(seq * PAD, PAD), PAD)
    own_values = [own_in[:, l].reshape(src_rows, HEAD_DIM) for l in range(layers)]
    lines = []
    for l in range(layers):
        factor, summed, total = partial[l]
        value = jnp.dot(
            image_ws[l, at, :].astype(bf16), own_values[l], preferred_element_type=f32
        )
        result = (summed + factor * value) / total
        lines.append(jnp.concatenate([result[h:h + 1] for h in range(group)], axis=1))
    att_ref[...] = jnp.concatenate(lines, axis=0).astype(bf16)
    moved = jnp.dot(
        put, jnp.concatenate(own_values, axis=1), preferred_element_type=f32
    ).astype(bf16)
    for l in range(layers):
        cache[l, 0, :, lanes_of(0)] = moved[:, l * HEAD_DIM:(l + 1) * HEAD_DIM]

    for l in range(layers):
        for k, hop in enumerate(hops):
            main_copy(l, k, hop).wait_send()
        for d in range(1, seq_count):
            part_copy(l, d).wait_send()
    for k, hop in enumerate(hops):
        own_copy(k, hop).wait_send()
        place_copy(k, hop).wait_send()


def finish(att_ref, cache_ref, att_out, cache_out, sem, small_sem):
    layers, pieces = sem.shape
    step = cache_ref.shape[2] // pieces
    copies = [
        pltpu.make_async_copy(
            cache_ref.at[l, :, i * step:(i + 1) * step],
            cache_out.at[l, :, i * step:(i + 1) * step],
            sem.at[l, i],
        )
        for l in range(layers)
        for i in range(pieces)
    ]
    copies.append(pltpu.make_async_copy(att_ref, att_out, small_sem.at[0]))
    for copy in copies:
        copy.start()
    for copy in copies:
        copy.wait()


def body(dims, query, text_cache, text_len, image_rows, patch_map, image_places):
    patch_count, seq_count, req_count = dims
    layers, req_dev, query_width = query.shape
    text_dev, full = text_cache.shape[2:]
    src_rows = image_rows.shape[1]
    groups = patch_count * req_count
    assert req_dev == 1 and seq_count == KV_HEADS and full == 2 * KV_HEADS * HEAD_DIM
    per = src_rows // groups
    hops = groups - 1
    kvw = full // 2
    main_width = full - HEAD_DIM
    rows_padded = KV_HEADS * PAD
    bf16, f32, i32 = jnp.bfloat16, jnp.float32, jnp.int32
    dma = pltpu.SemaphoreType.DMA
    vmem = pl.BlockSpec(memory_space=pltpu.VMEM)
    hbm = pl.BlockSpec(memory_space=pltpu.HBM)
    att_shape = jax.ShapeDtypeStruct((layers, query_width // seq_count), bf16)
    cache_shape = jax.ShapeDtypeStruct((layers, 1, src_rows, full), bf16)
    in_hbm = lambda x: pltpu.with_memory_space_constraint(x, pltpu.HBM)
    in_vmem = lambda x: pltpu.with_memory_space_constraint(x, pltpu.VMEM)
    attended, cache = pl.pallas_call(
        functools.partial(kernel, dims),
        out_shape=(
            pltpu.VMEM(att_shape.shape, bf16), pltpu.VMEM(cache_shape.shape, bf16)
        ),
        in_specs=[hbm, pl.BlockSpec(memory_space=pl.ANY), hbm, hbm, hbm, hbm],
        out_specs=(vmem, vmem),
        scratch_shapes=[
            pltpu.VMEM((layers, query_width), bf16),
            pltpu.VMEM((PAD, HEAD_DIM), i32),
            pltpu.VMEM((1, src_rows), i32),
            pltpu.VMEM((1, src_rows), i32),
            pltpu.VMEM((layers, src_rows, full), bf16),
            pltpu.VMEM((layers, text_dev, full), bf16),
            pltpu.VMEM((layers, groups, per, main_width), bf16),
            pltpu.VMEM((layers, groups, per, main_width), bf16),
            pltpu.VMEM((groups, layers, per, HEAD_DIM), bf16),
            pltpu.VMEM((groups, layers, per, HEAD_DIM), bf16),
            pltpu.VMEM((1, src_rows), i32),
            pltpu.VMEM((groups, 1, src_rows), i32),
            pltpu.VMEM((layers, rows_padded, text_dev), f32),
            pltpu.VMEM((layers, rows_padded, src_rows), f32),
            pltpu.VMEM((rows_padded, kvw + 2 * HEAD_DIM), f32),
            pltpu.VMEM((rows_padded, main_width - kvw), f32),
            pltpu.VMEM((layers, seq_count, PAD, 3 * HEAD_DIM), f32),
            pltpu.VMEM((layers, seq_count, PAD, 3 * HEAD_DIM), f32),
            dma((4,)), dma((layers,)), dma((layers,)),
            dma((layers, hops)), dma((layers, hops)), dma((hops,)), dma((hops,)),
            dma((hops,)), dma((hops,)), dma((layers, seq_count)), dma((layers, seq_count)),
        ],
        compiler_params=pltpu.CompilerParams(
            collective_id=0, has_side_effects=True, vmem_limit_bytes=32 * 1024 * 1024
        ),
    )(
        in_hbm(query.reshape(layers, query_width)), jnp.broadcast_to(text_len.reshape(1, 1), (PAD, HEAD_DIM)),
        in_hbm(patch_map.reshape(1, src_rows)), in_hbm(image_places.reshape(1, src_rows)),
        in_hbm(image_rows), in_hbm(text_cache),
    )
    attended, cache = pl.pallas_call(
        finish,
        out_shape=(att_shape, cache_shape),
        in_specs=[vmem, vmem],
        out_specs=(hbm, hbm),
        scratch_shapes=[dma((layers, 4)), dma((1,))],
    )(in_vmem(attended), in_vmem(cache))
    return attended.reshape(layers, 1, query_width // seq_count), cache


def solution(mesh):
    dims = tuple(mesh.shape[a] for a in ("patch", "seq", "req"))
    return jax.shard_map(
        functools.partial(body, dims),
        mesh=mesh,
        in_specs=(
            P(None, ("patch", "req"), None),
            P(None, ("patch", "req"), "seq", None),
            P(("patch", "req")),
            P(None, ("patch", "seq", "req"), None),
            P(("patch", "seq", "req")),
            P(("patch", "seq", "req")),
        ),
        out_specs=(P(None, ("patch", "req"), "seq"), P(None, ("patch", "req"), "seq", None)),
        check_vma=False,
    )
```

profile of v0, /device:TPU:9, one launch (start us, length us, event | category | flops | bytes accessed | tf_op | source)
XLA Modules:
  0.0 55.3 jit_solution(1955004564856247076)
XLA Ops:
  1.3 52.6 %shard_map.77 = (bf16[4,896]{1,0:T(4,128)(2,1)S(1)}, bf16[4,1,256,1024]{3,2,1,0:T(8,128)(2,1)S(1)}) custom-call(bf16[4,3584]{1,0:T(4,128)(2,1)} %bitcast.6, s32[8,128]{1,0:T(8,128)S(1)} %broadcast_in_dim.8.len_hbm, s32[1,256]{1,0:T(1,128)} %bitcast.7, s32[1,256]{1,0:T(1,128)} %bitcast.8, bf16[4,256,1024]{2,1,0:T(8,128)(2,1)} %rows_hbm.1, ...), custom_call_target="tpu_custom_call" | custom-call | tf_op jit(solution)/shard_map/pallas_call | solution.py:328
  53.9 1.5 %shard_map.78 = (bf16[4,896]{1,0:T(4,128)(2,1)}, bf16[4,1,256,1024]{3,2,1,0:T(8,128)(2,1)}) custom-call(bf16[4,896]{1,0:T(4,128)(2,1)S(1)} %get-tuple-element.6.att_ref, bf16[4,1,256,1024]{3,2,1,0:T(8,128)(2,1)S(1)} %get-tuple-element.7.cache_ref), custom_call_target="tpu_custom_call" | custom-call | tf_op jit(solution)/shard_map/pallas_call | solution.py:366
  (1 shorter events, 0.0 us)
where the time goes:
time: 55.5 us; the launch traced here: 55.3 us
  Pallas kernels  54 us (97%)
  between operations  1.29 us (2%)
    pallas_call x1, Pallas kernels, body(): pl.pallas_call(functools.partial(kernel, dims), out_shape=(pltpu.VMEM(att...  52.6 us
    pallas_call x1, Pallas kernels, body(): pl.pallas_call(finish, out_shape=(att_shape, cache_shape), in_specs=[vmem...  1.45 us

commit v1 on v0

v1 whole, which is shorter than its diff:
```python
import functools
import math

import jax
import jax.numpy as jnp
from jax import lax
from jax.experimental import pallas as pl
from jax.experimental.pallas import tpu as pltpu
from jax.sharding import PartitionSpec as P

HEADS = 28
KV_HEADS = 4
HEAD_DIM = 128
PAD = 8
MESH = pl.DeviceIdType.MESH
NT = (((1,), (1,)), ((), ()))


def near_hops(patch_count, req_count):
    half = patch_count // 2
    beside = [("near", i, c) for i in range(1, half) for c in range(req_count)]
    return beside + [("near", 0, c) for c in range(1, req_count)]


def far_hops(patch_count, req_count, k):
    return [("far", k, c) for c in range(req_count)]


def exchange(
    dims,
    query_hbm, len_hbm, map_hbm, place_hbm, rows_hbm, text_hbm,
    cache, put_out, values_out, weights_out, partial_out,
    query, length, maps, places, rows, text, main_out, main_in, own_out, own_in, place_out, place_in,
    heads, scores, part_out, part_in,
    small_sem, rows_sem, text_sem, main_send, main_recv, own_send, own_recv,
    place_send, place_recv, part_send, part_recv,
):
    patch_count, seq_count, req_count = dims
    layers, src_rows, full = rows.shape
    text_dev = text.shape[1]
    kvw = full // 2
    group = HEADS // KV_HEADS
    groups = patch_count * req_count
    per = src_rows // groups
    half = patch_count // 2
    side = (seq_count - 1) * HEAD_DIM
    main_width = 2 * side
    scale = 1.0 / math.sqrt(HEAD_DIM)
    patch, seq, req = (lax.axis_index(a) for a in ("patch", "seq", "req"))
    me = patch * req_count + req
    near = near_hops(patch_count, req_count)
    far = [far_hops(patch_count, req_count, k) for k in range(half)]
    hops = near + [hop for wave in far for hop in wave]
    f32, bf16 = jnp.float32, jnp.bfloat16
    upper = patch // half

    def partner(hop):
        kind, i, c = hop
        r = lax.rem(req + c, req_count)
        if kind == "near":
            return upper * half + lax.rem(lax.rem(patch, half) + i, half), r
        return (1 - upper) * (patch_count - 1 - i) + upper * i, r

    def rows_copy(l):
        return pltpu.make_async_copy(rows_hbm.at[l], rows.at[l], rows_sem.at[l])

    def text_copy(l):
        return pltpu.make_async_copy(text_hbm.at[l, 0], text.at[l], text_sem.at[l])

    small = [
        pltpu.make_async_copy(map_hbm, maps, small_sem.at[0]),
        pltpu.make_async_copy(place_hbm, places, small_sem.at[1]),
        pltpu.make_async_copy(query_hbm, query, small_sem.at[2]),
        pltpu.make_async_copy(len_hbm, length, small_sem.at[3]),
    ]
    small[0].start()
    rows_copy(0).start()
    barrier = pltpu.get_barrier_semaphore()
    for hop in hops:
        p, r = partner(hop)
        pl.semaphore_signal(barrier, inc=1, device_id=(p, seq, r), device_id_type=MESH)
    for d in range(1, seq_count):
        s = lax.rem(seq + d, seq_count)
        pl.semaphore_signal(barrier, inc=1, device_id=(patch, s, req), device_id_type=MESH)
    for copy in small[1:]:
        copy.start()

    def lanes_of(d, base=0):
        g = lax.rem(seq + d, seq_count)
        return pl.ds(pl.multiple_of(base + g * HEAD_DIM, HEAD_DIM), HEAD_DIM)

    owner = lax.broadcasted_iota(jnp.int32, (groups, src_rows), 0)
    row_i = lax.broadcasted_iota(jnp.int32, (src_rows, src_rows), 0)
    col_i = lax.broadcasted_iota(jnp.int32, (src_rows, src_rows), 1)
    before = (row_i < col_i).astype(f32).astype(bf16)
    small[0].wait()
    mine = maps[...] == owner
    rank = jnp.dot(mine.astype(f32).astype(bf16), before, preferred_element_type=f32)
    slot = jnp.sum(
        jnp.where(mine, rank + (owner * per).astype(f32), 0.0), axis=0, keepdims=True
    )
    pick = (row_i == slot.astype(jnp.int32)).astype(f32).astype(bf16)

    def place_copy(hop):
        p, r = partner(hop)
        q = p * req_count + r
        return pltpu.make_async_remote_copy(
            src_ref=place_out, dst_ref=place_in.at[me],
            send_sem=place_send.at[q], recv_sem=place_recv.at[me],
            device_id=(p, seq, r), device_id_type=MESH,
        )

    def place_wait(hop):
        p, r = partner(hop)
        q = p * req_count + r
        pltpu.make_async_remote_copy(
            src_ref=place_out, dst_ref=place_in.at[q],
            send_sem=place_send.at[q], recv_sem=place_recv.at[q],
            device_id=(p, seq, r), device_id_type=MESH,
        ).wait_recv()

    def main_copy(l, hop):
        p, r = partner(hop)
        q = p * req_count + r
        return pltpu.make_async_remote_copy(
            src_ref=main_out.at[l, q], dst_ref=main_in.at[l, me],
            send_sem=main_send.at[l, q], recv_sem=main_recv.at[l, me],
            device_id=(p, seq, r), device_id_type=MESH,
        )

    def main_wait(l, hop):
        p, r = partner(hop)
        q = p * req_count + r
        pltpu.make_async_remote_copy(
            src_ref=main_out.at[l, q], dst_ref=main_in.at[l, q],
            send_sem=main_send.at[l, q], recv_sem=main_recv.at[l, q],
            device_id=(p, seq, r), device_id_type=MESH,
        ).wait_recv()

    def own_copy(i, hop):
        p, r = partner(hop)
        q = p * req_count + r
        return pltpu.make_async_remote_copy(
            src_ref=own_out.at[i, q], dst_ref=own_in.at[i, me],
            send_sem=own_send.at[i, q], recv_sem=own_recv.at[i, me],
            device_id=(p, seq, r), device_id_type=MESH,
        )

    def own_wait(i, hop):
        p, r = partner(hop)
        q = p * req_count + r
        pltpu.make_async_remote_copy(
            src_ref=own_out.at[i, q], dst_ref=own_in.at[i, q],
            send_sem=own_send.at[i, q], recv_sem=own_recv.at[i, q],
            device_id=(p, seq, r), device_id_type=MESH,
        ).wait_recv()

    def part_copy(l, d):
        s = lax.rem(seq + d, seq_count)
        return pltpu.make_async_remote_copy(
            src_ref=part_out.at[l, d], dst_ref=part_in.at[l, d],
            send_sem=part_send.at[l, d], recv_sem=part_recv.at[l, d],
            device_id=(patch, s, req), device_id_type=MESH,
        )

    for l in range(layers):
        rows_copy(l).wait()
        if l == 0:
            for m in range(1, layers):
                rows_copy(m).start()
        turned = jnp.concatenate(
            [rows[l, :, lanes_of(d)] for d in range(1, seq_count)]
            + [rows[l, :, lanes_of(d, kvw)] for d in range(1, seq_count)],
            axis=1,
        )
        moved = jnp.dot(pick, turned, preferred_element_type=f32).astype(bf16)
        main_out[l] = moved.reshape(groups, per, main_width)
        if l == 0:
            pl.semaphore_wait(barrier, len(hops) + seq_count - 1)
        for hop in near:
            main_copy(l, hop).start()
        for wave in far[:-1]:
            for hop in wave:
                main_copy(l, hop).start()
        if l == 0:
            small[1].wait()
            local = (places[...] - seq * src_rows).astype(f32).astype(bf16)
            place_sorted = lax.dot_general(
                jnp.broadcast_to(local, (PAD, src_rows)), pick, NT,
                preferred_element_type=f32,
            )
            place_out[...] = place_sorted[0:1].astype(jnp.int32)
            place_in[me] = place_sorted[0:1].astype(jnp.int32)
            for hop in hops:
                place_copy(hop).start()
    for l in range(layers):
        turned = jnp.concatenate([rows[l, :, lanes_of(0)], rows[l, :, lanes_of(0, kvw)]], axis=1)
        moved = jnp.dot(pick, turned, preferred_element_type=f32).astype(bf16)
        own_out[0, :, l] = moved[:, :HEAD_DIM].reshape(groups, per, HEAD_DIM)
        own_out[1, :, l] = moved[:, HEAD_DIM:].reshape(groups, per, HEAD_DIM)
    for i in range(2):
        for hop in near:
            own_copy(i, hop).start()
    for l in range(layers):
        for hop in far[-1]:
            main_copy(l, hop).start()
    for wave in far:
        for i in range(2):
            for hop in wave:
                own_copy(i, hop).start()
    for l in range(layers):
        text_copy(l).start()
    for l in range(layers):
        main_in[l, me] = main_out[l, me]
    for i in range(2):
        own_in[i, me] = own_out[i, me]

    small[2].wait()
    lines = query[...].astype(f32)
    for l in range(layers):
        for g in range(KV_HEADS):
            heads[l, g * PAD:(g + 1) * PAD, :] = jnp.concatenate(
                [
                    lines[l:l + 1, (g * group + h) * HEAD_DIM:(g * group + h + 1) * HEAD_DIM]
                    for h in range(group)
                ] + [jnp.zeros((PAD - group, HEAD_DIM), f32)],
                axis=0,
            )

    def head_block(l, d):
        g = lax.rem(seq + d, seq_count)
        return heads[l, pl.ds(pl.multiple_of(g * PAD, PAD), PAD), :]

    small[3].wait()
    positions = seq * text_dev + lax.broadcasted_iota(
        jnp.int32, (KV_HEADS * PAD, text_dev), 1
    )
    used = positions < length[0]
    lane_group = lax.broadcasted_iota(jnp.int32, (PAD, kvw), 1) // HEAD_DIM
    for l in range(layers):
        spread = jnp.concatenate(
            [
                jnp.where(
                    lane_group == lax.rem(seq + d, seq_count),
                    jnp.concatenate([head_block(l, d)] * KV_HEADS, axis=1),
                    0.0,
                )
                for d in range(seq_count)
            ],
            axis=0,
        ).astype(bf16)
        text_copy(l).wait()
        raw = lax.dot_general(
            spread, text[l, :, :kvw], NT, preferred_element_type=f32
        ) * scale
        scores[l] = jnp.where(used, raw, -jnp.inf)

    for hop in hops:
        place_wait(hop)
    wanted = (row_i == me * per + lax.rem(col_i, per)).astype(f32).astype(bf16)
    lanes = jnp.dot(
        place_in[...].reshape(groups, src_rows).astype(f32).astype(bf16), wanted,
        preferred_element_type=f32,
    )
    source = lax.broadcasted_iota(jnp.int32, (groups, src_rows), 1) // per
    place = jnp.sum(jnp.where(source == owner, lanes, 0.0), axis=0, keepdims=True)
    put = (row_i == place.astype(jnp.int32)).astype(f32).astype(bf16)
    put_out[...] = put

    zeros = jnp.zeros((PAD, HEAD_DIM), f32)
    for l in range(layers):
        spread = jnp.concatenate(
            [
                jnp.concatenate(
                    [head_block(l, d) if c == d else zeros for c in range(1, seq_count)],
                    axis=1,
                )
                for d in range(1, seq_count)
            ],
            axis=0,
        ).astype(bf16)
        for hop in hops:
            main_wait(l, hop)
        block = main_in[l].reshape(src_rows, main_width)
        image_scores = lax.dot_general(
            spread, block[:, :side], NT, preferred_element_type=f32
        ) * scale
        text_scores = scores[l, PAD:, :]
        top = jnp.maximum(
            jnp.max(text_scores, axis=1, keepdims=True),
            jnp.max(image_scores, axis=1, keepdims=True),
        )
        text_w = jnp.exp(text_scores - top)
        image_w = jnp.exp(image_scores - top)
        total = jnp.sum(text_w, axis=1, keepdims=True) + jnp.sum(
            image_w, axis=1, keepdims=True
        )
        image_sums = jnp.dot(
            image_w.astype(bf16), block[:, side:], preferred_element_type=f32
        )
        for d in range(1, seq_count):
            at = slice((d - 1) * PAD, d * PAD)
            text_sums = jnp.dot(
                text_w[at].astype(bf16), text[l, :, lanes_of(d, kvw)],
                preferred_element_type=f32,
            )
            part_out[l, d, :, :HEAD_DIM] = (
                text_sums + image_sums[at, (d - 1) * HEAD_DIM:d * HEAD_DIM]
            )
            part_out[l, d, :, HEAD_DIM:2 * HEAD_DIM] = jnp.broadcast_to(
                top[at], (PAD, HEAD_DIM)
            )
            part_out[l, d, :, 2 * HEAD_DIM:] = jnp.broadcast_to(total[at], (PAD, HEAD_DIM))
            part_copy(l, d).start()
        moved = jnp.dot(put, block, preferred_element_type=f32).astype(bf16)
        for d in range(1, seq_count):
            cache[l, 0, :, lanes_of(d)] = moved[:, (d - 1) * HEAD_DIM:d * HEAD_DIM]
            cache[l, 0, :, lanes_of(d, kvw)] = moved[
                :, side + (d - 1) * HEAD_DIM:side + d * HEAD_DIM
            ]

    for hop in hops:
        own_wait(0, hop)
    own_keys = [own_in[0, :, l].reshape(src_rows, HEAD_DIM) for l in range(layers)]
    mine_now = []
    for l in range(layers):
        image_scores = lax.dot_general(
            head_block(l, 0).astype(bf16), own_keys[l], NT, preferred_element_type=f32
        ) * scale
        text_scores = scores[l, :PAD, :]
        top = jnp.maximum(
            jnp.max(text_scores, axis=1, keepdims=True),
            jnp.max(image_scores, axis=1, keepdims=True),
        )
        text_w = jnp.exp(text_scores - top)
        image_w = jnp.exp(image_scores - top)
        total = jnp.sum(text_w, axis=1, keepdims=True) + jnp.sum(
            image_w, axis=1, keepdims=True
        )
        value = jnp.dot(
            text_w.astype(bf16), text[l, :, lanes_of(0, kvw)], preferred_element_type=f32
        )
        weights_out[l * PAD:(l + 1) * PAD, :] = image_w
        mine_now.append(
            (value, jnp.broadcast_to(top, (PAD, HEAD_DIM)), jnp.broadcast_to(total, (PAD, HEAD_DIM)))
        )
    moved = jnp.dot(
        put, jnp.concatenate(own_keys, axis=1), preferred_element_type=f32
    ).astype(bf16)
    for l in range(layers):
        cache[l, 0, :, lanes_of(0)] = moved[:, l * HEAD_DIM:(l + 1) * HEAD_DIM]

    for l in range(layers):
        for d in range(1, seq_count):
            part_copy(l, d).wait_recv()
        cells = [mine_now[l]] + [
            tuple(part_in[l, d, :, i * HEAD_DIM:(i + 1) * HEAD_DIM] for i in range(3))
            for d in range(1, seq_count)
        ]
        top = functools.reduce(jnp.maximum, [c[1] for c in cells])
        factors = [jnp.exp(c[1] - top) for c in cells]
        partial_out[l, :, :HEAD_DIM] = factors[0]
        partial_out[l, :, HEAD_DIM:2 * HEAD_DIM] = sum(
            f * c[0] for f, c in zip(factors, cells)
        )
        partial_out[l, :, 2 * HEAD_DIM:] = sum(f * c[2] for f, c in zip(factors, cells))

    for l in range(layers):
        for hop in hops:
            main_copy(l, hop).wait_send()
        for d in range(1, seq_count):
            part_copy(l, d).wait_send()
    for hop in hops:
        place_copy(hop).wait_send()
        own_copy(0, hop).wait_send()
    for hop in hops:
        own_wait(1, hop)
    for l in range(layers):
        values_out[:, l * HEAD_DIM:(l + 1) * HEAD_DIM] = own_in[1, :, l].reshape(
            src_rows, HEAD_DIM
        )
    for hop in hops:
        own_copy(1, hop).wait_send()


def finish(
    dims, cache, put, values, weights, partial, att_out, cache_out, att, last, sem, last_sem
):
    _, seq_count, _ = dims
    layers, _, src_rows, full = cache.shape
    kvw = full // 2
    group = HEADS // KV_HEADS
    seq = lax.axis_index("seq")
    f32, bf16 = jnp.float32, jnp.bfloat16

    def lanes_of(d):
        g = lax.rem(seq + d, seq_count)
        return pl.ds(pl.multiple_of(kvw + g * HEAD_DIM, HEAD_DIM), HEAD_DIM)

    early = []
    for l in range(layers):
        early.append(
            pltpu.make_async_copy(
                cache.at[l, 0, :, pl.ds(0, kvw)], cache_out.at[l, 0, :, pl.ds(0, kvw)],
                sem.at[l, 0],
            )
        )
        for d in range(1, seq_count):
            early.append(
                pltpu.make_async_copy(
                    cache.at[l, 0, :, lanes_of(d)], cache_out.at[l, 0, :, lanes_of(d)],
                    sem.at[l, d],
                )
            )
    for copy in early:
        copy.start()
    late = []
    both = jnp.concatenate([put[...], weights[...].astype(bf16)], axis=0)
    moved = jnp.dot(both, values[...], preferred_element_type=f32)
    for l in range(layers):
        at = slice(l * HEAD_DIM, (l + 1) * HEAD_DIM)
        last[l] = moved[:src_rows, at].astype(bf16)
        late.append(
            pltpu.make_async_copy(
                last.at[l], cache_out.at[l, 0, :, lanes_of(0)], last_sem.at[l]
            )
        )
        late[-1].start()
    lines = []
    for l in range(layers):
        value = moved[
            src_rows + l * PAD:src_rows + (l + 1) * PAD, l * HEAD_DIM:(l + 1) * HEAD_DIM
        ]
        factor = partial[l, :, :HEAD_DIM]
        summed = partial[l, :, HEAD_DIM:2 * HEAD_DIM]
        result = (summed + factor * value) / partial[l, :, 2 * HEAD_DIM:]
        lines.append(jnp.concatenate([result[h:h + 1] for h in range(group)], axis=1))
    att[...] = jnp.concatenate(lines, axis=0).astype(bf16)
    late.append(pltpu.make_async_copy(att, att_out, last_sem.at[layers]))
    late[-1].start()
    for copy in early + late:
        copy.wait()


def body(dims, query, text_cache, text_len, image_rows, patch_map, image_places):
    patch_count, seq_count, req_count = dims
    layers, req_dev, query_width = query.shape
    text_dev, full = text_cache.shape[2:]
    src_rows = image_rows.shape[1]
    groups = patch_count * req_count
    assert req_dev == 1 and seq_count == KV_HEADS and full == 2 * KV_HEADS * HEAD_DIM
    assert patch_count % 2 == 0
    per = src_rows // groups
    main_width = full - 2 * HEAD_DIM
    rows_padded = KV_HEADS * PAD
    bf16, f32, i32 = jnp.bfloat16, jnp.float32, jnp.int32
    dma = pltpu.SemaphoreType.DMA
    vmem = pl.BlockSpec(memory_space=pltpu.VMEM)
    hbm = pl.BlockSpec(memory_space=pltpu.HBM)
    att_shape = jax.ShapeDtypeStruct((layers, query_width // seq_count), bf16)
    cache_shape = jax.ShapeDtypeStruct((layers, 1, src_rows, full), bf16)
    in_hbm = lambda x: pltpu.with_memory_space_constraint(x, pltpu.HBM)
    in_vmem = lambda x: pltpu.with_memory_space_constraint(x, pltpu.VMEM)
    state = pl.pallas_call(
        functools.partial(exchange, dims),
        out_shape=(
            pltpu.VMEM(cache_shape.shape, bf16),
            pltpu.VMEM((src_rows, src_rows), bf16),
            pltpu.VMEM((src_rows, layers * HEAD_DIM), bf16),
            pltpu.VMEM((layers * PAD, src_rows), f32),
            pltpu.VMEM((layers, PAD, 3 * HEAD_DIM), f32),
        ),
        in_specs=[hbm, pl.BlockSpec(memory_space=pl.ANY), hbm, hbm, hbm, hbm],
        out_specs=(vmem,) * 5,
        scratch_shapes=[
            pltpu.VMEM((layers, query_width), bf16),
            pltpu.SMEM((1,), i32),
            pltpu.VMEM((1, src_rows), i32),
            pltpu.VMEM((1, src_rows), i32),
            pltpu.VMEM((layers, src_rows, full), bf16),
            pltpu.VMEM((layers, text_dev, full), bf16),
            pltpu.VMEM((layers, groups, per, main_width), bf16),
            pltpu.VMEM((layers, groups, per, main_width), bf16),
            pltpu.VMEM((2, groups, layers, per, HEAD_DIM), bf16),
            pltpu.VMEM((2, groups, layers, per, HEAD_DIM), bf16),
            pltpu.VMEM((1, src_rows), i32),
            pltpu.VMEM((groups, 1, src_rows), i32),
            pltpu.VMEM((layers, rows_padded, HEAD_DIM), f32),
            pltpu.VMEM((layers, rows_padded, text_dev), f32),
            pltpu.VMEM((layers, seq_count, PAD, 3 * HEAD_DIM), f32),
            pltpu.VMEM((layers, seq_count, PAD, 3 * HEAD_DIM), f32),
            dma((4,)), dma((layers,)), dma((layers,)),
            dma((layers, groups)), dma((layers, groups)), dma((2, groups)), dma((2, groups)),
            dma((groups,)), dma((groups,)), dma((layers, seq_count)), dma((layers, seq_count)),
        ],
        compiler_params=pltpu.CompilerParams(
            collective_id=0, has_side_effects=True, vmem_limit_bytes=32 * 1024 * 1024
        ),
    )(
        in_hbm(query.reshape(layers, query_width)), text_len,
        in_hbm(patch_map.reshape(1, src_rows)), in_hbm(image_places.reshape(1, src_rows)),
        in_hbm(image_rows), in_hbm(text_cache),
    )
    attended, cache = pl.pallas_call(
        functools.partial(finish, dims),
        out_shape=(att_shape, cache_shape),
        in_specs=[vmem] * 5,
        out_specs=(hbm, hbm),
        scratch_shapes=[
            pltpu.VMEM(att_shape.shape, bf16),
            pltpu.VMEM((layers, src_rows, HEAD_DIM), bf16),
            dma((layers, seq_count)), dma((layers + 1,)),
        ],
    )(*(in_vmem(x) for x in state))
    return attended.reshape(layers, 1, query_width // seq_count), cache


def solution(mesh):
    dims = tuple(mesh.shape[a] for a in ("patch", "seq", "req"))
    return jax.shard_map(
        functools.partial(body, dims),
        mesh=mesh,
        in_specs=(
            P(None, ("patch", "req"), None),
            P(None, ("patch", "req"), "seq", None),
            P(("patch", "req")),
            P(None, ("patch", "seq", "req"), None),
            P(("patch", "seq", "req")),
            P(("patch", "seq", "req")),
        ),
        out_specs=(P(None, ("patch", "req"), "seq"), P(None, ("patch", "req"), "seq", None)),
        check_vma=False,
    )
```

time: 55.5 us -> 54.5 us (0.982)
  Pallas kernels: 54 us -> 53.1 us
    pallas_call x2, Pallas kernels: 54 us -> 53.1 us  [the longest x1 51.6 us: body(): pl.pallas_call(functools.partial(exchange, dims), out_shape=(pltpu.VMEM(c...]
where the time goes in v1:
time: 54.5 us; the launch traced here: 54.3 us
  Pallas kernels  53.1 us (97%)
  between operations  1.28 us (2%)
    pallas_call x1, Pallas kernels, body(): pl.pallas_call(functools.partial(exchange, dims), out_shape=(pltpu.VMEM(c...  51.6 us
    pallas_call x1, Pallas kernels, body(): pl.pallas_call(functools.partial(finish, dims), out_shape=(att_shape, cac...  1.51 us

profile of v1, /device:TPU:9, one launch (start us, length us, event | category | flops | bytes accessed | tf_op | source)
XLA Modules:
  0.0 54.3 jit_solution(9454255756770702803)
XLA Ops:
  1.3 51.6 %shard_map.77 = (bf16[4,1,256,1024]{3,2,1,0:T(8,128)(2,1)S(1)}, bf16[256,256]{1,0:T(8,128)(2,1)S(1)}, bf16[256,512]{1,0:T(8,128)(2,1)S(1)}, f32[32,256]{1,0:T(8,128)S(1)}, f32[4,8,384]{2,1,0:T(8,128)S(1)}) custom-call(bf16[4,3584]{1,0:T(4,128)(2,1)} %bitcast.4, s32[1]{0:T(128)S(6)} %copy.8.len_hbm, s32[1,256]{1,0:T(1,128)} %bitcast.5, s32[1,256]{1,0:T(1,128)} %bitcast.6, ...), custom_call_target="tpu_custom_call" | custom-call | tf_op jit(solution)/shard_map/pallas_call | solution.py:464
  52.8 1.5 %shard_map.78 = (bf16[4,896]{1,0:T(4,128)(2,1)}, bf16[4,1,256,1024]{3,2,1,0:T(8,128)(2,1)}) custom-call(bf16[4,1,256,1024]{3,2,1,0:T(8,128)(2,1)S(1)} %get-tuple-element.9.cache, bf16[256,256]{1,0:T(8,128)(2,1)S(1)} %get-tuple-element.10.put, bf16[256,512]{1,0:T(8,128)(2,1)S(1)} %get-tuple-element.11.values, f32[32,256]{1,0:T(8,128)S(1)} %get-tuple-element.12.weights, ...), custom_call_target="tpu_custom_call" | custom-call | tf_op jit(solution)/shard_map/pallas_call | solution.py:504

commit v2 on v1

--- a/solution.py
+++ b/solution.py
@@ -29,11 +29,10 @@
 def exchange(
     dims,
     query_hbm, len_hbm, map_hbm, place_hbm, rows_hbm, text_hbm,
-    cache, put_out, values_out, weights_out, partial_out,
-    query, length, maps, places, rows, text, main_out, main_in, own_out, own_in, place_out, place_in,
+    cache, put_out, values_in, weights_out, partial_out,
+    query, length, maps, places, rows, text, main_out, main_in, own_out, keys_in, place_out, place_in,
     heads, scores, part_out, part_in,
-    small_sem, rows_sem, text_sem, main_send, main_recv, own_send, own_recv,
-    place_send, place_recv, part_send, part_recv,
+    small_sem, rows_sem, text_sem, main_send, main_recv, own_send, own_recv, place_sem, part_sem,
 ):
     patch_count, seq_count, req_count = dims
     layers, src_rows, full = rows.shape
@@ -61,11 +60,15 @@
             return upper * half + lax.rem(lax.rem(patch, half) + i, half), r
         return (1 - upper) * (patch_count - 1 - i) + upper * i, r
 
-    def rows_copy(l):
-        return pltpu.make_async_copy(rows_hbm.at[l], rows.at[l], rows_sem.at[l])
-
-    def text_copy(l):
-        return pltpu.make_async_copy(text_hbm.at[l, 0], text.at[l], text_sem.at[l])
+    others = pl.ds(0, groups - 1)
+    own_in = (keys_in, values_in)
+    first_rows = pltpu.make_async_copy(rows_hbm.at[0], rows.at[0], rows_sem.at[0])
+    later = pl.ds(1, layers - 1)
+    later_rows = pltpu.make_async_copy(rows_hbm.at[later], rows.at[later], rows_sem.at[1])
+    text_copy = pltpu.make_async_copy(text_hbm.at[:, 0], text, text_sem.at[0])
+
+    def settle(ref, sem):
+        pltpu.make_async_copy(ref, ref, sem).wait()
 
     small = [
         pltpu.make_async_copy(map_hbm, maps, small_sem.at[0]),
@@ -74,7 +77,7 @@
         pltpu.make_async_copy(len_hbm, length, small_sem.at[3]),
     ]
     small[0].start()
-    rows_copy(0).start()
+    first_rows.start()
     barrier = pltpu.get_barrier_semaphore()
     for hop in hops:
         p, r = partner(hop)
@@ -103,71 +106,42 @@
 
     def place_copy(hop):
         p, r = partner(hop)
-        q = p * req_count + r
         return pltpu.make_async_remote_copy(
             src_ref=place_out, dst_ref=place_in.at[me],
-            send_sem=place_send.at[q], recv_sem=place_recv.at[me],
+            send_sem=place_sem.at[0], recv_sem=place_sem.at[1],
             device_id=(p, seq, r), device_id_type=MESH,
         )
-
-    def place_wait(hop):
-        p, r = partner(hop)
-        q = p * req_count + r
-        pltpu.make_async_remote_copy(
-            src_ref=place_out, dst_ref=place_in.at[q],
-            send_sem=place_send.at[q], recv_sem=place_recv.at[q],
-            device_id=(p, seq, r), device_id_type=MESH,
-        ).wait_recv()
 
     def main_copy(l, hop):
         p, r = partner(hop)
-        q = p * req_count + r
         return pltpu.make_async_remote_copy(
-            src_ref=main_out.at[l, q], dst_ref=main_in.at[l, me],
-            send_sem=main_send.at[l, q], recv_sem=main_recv.at[l, me],
+            src_ref=main_out.at[l, p * req_count + r], dst_ref=main_in.at[l, me],
+            send_sem=main_send.at[0], recv_sem=main_recv.at[l],
             device_id=(p, seq, r), device_id_type=MESH,
         )
-
-    def main_wait(l, hop):
-        p, r = partner(hop)
-        q = p * req_count + r
-        pltpu.make_async_remote_copy(
-            src_ref=main_out.at[l, q], dst_ref=main_in.at[l, q],
-            send_sem=main_send.at[l, q], recv_sem=main_recv.at[l, q],
-            device_id=(p, seq, r), device_id_type=MESH,
-        ).wait_recv()
 
     def own_copy(i, hop):
         p, r = partner(hop)
-        q = p * req_count + r
         return pltpu.make_async_remote_copy(
-            src_ref=own_out.at[i, q], dst_ref=own_in.at[i, me],
-            send_sem=own_send.at[i, q], recv_sem=own_recv.at[i, me],
+            src_ref=own_out.at[i, p * req_count + r], dst_ref=own_in[i].at[me],
+            send_sem=own_send.at[0], recv_sem=own_recv.at[i],
             device_id=(p, seq, r), device_id_type=MESH,
         )
-
-    def own_wait(i, hop):
-        p, r = partner(hop)
-        q = p * req_count + r
-        pltpu.make_async_remote_copy(
-            src_ref=own_out.at[i, q], dst_ref=own_in.at[i, q],
-            send_sem=own_send.at[i, q], recv_sem=own_recv.at[i, q],
-            device_id=(p, seq, r), device_id_type=MESH,
-        ).wait_recv()
 
     def part_copy(l, d):
         s = lax.rem(seq + d, seq_count)
         return pltpu.make_async_remote_copy(
             src_ref=part_out.at[l, d], dst_ref=part_in.at[l, d],
-            send_sem=part_send.at[l, d], recv_sem=part_recv.at[l, d],
+            send_sem=part_sem.at[0], recv_sem=part_sem.at[1],
             device_id=(patch, s, req), device_id_type=MESH,
         )
 
     for l in range(layers):
-        rows_copy(l).wait()
         if l == 0:
-            for m in range(1, layers):
-                rows_copy(m).start()
+            first_rows.wait()
+            later_rows.start()
+        if l == 1:
+            later_rows.wait()
         turned = jnp.concatenate(
             [rows[l, :, lanes_of(d)] for d in range(1, seq_count)]
             + [rows[l, :, lanes_of(d, kvw)] for d in range(1, seq_count)],
@@ -208,12 +182,11 @@
         for i in range(2):
             for hop in wave:
                 own_copy(i, hop).start()
-    for l in range(layers):
-        text_copy(l).start()
+    text_copy.start()
     for l in range(layers):
         main_in[l, me] = main_out[l, me]
     for i in range(2):
-        own_in[i, me] = own_out[i, me]
+        own_in[i][me] = own_out[i, me]
 
     small[2].wait()
     lines = query[...].astype(f32)
@@ -249,14 +222,14 @@
             ],
             axis=0,
         ).astype(bf16)
-        text_copy(l).wait()
+        if l == 0:
+            text_copy.wait()
         raw = lax.dot_general(
             spread, text[l, :, :kvw], NT, preferred_element_type=f32
         ) * scale
         scores[l] = jnp.where(used, raw, -jnp.inf)
 
-    for hop in hops:
-        place_wait(hop)
+    settle(place_in.at[others], place_sem.at[1])
     wanted = (row_i == me * per + lax.rem(col_i, per)).astype(f32).astype(bf16)
     lanes = jnp.dot(
         place_in[...].reshape(groups, src_rows).astype(f32).astype(bf16), wanted,
@@ -279,8 +252,7 @@
             ],
             axis=0,
         ).astype(bf16)
-        for hop in hops:
-            main_wait(l, hop)
+        settle(main_in.at[l, others], main_recv.at[l])
         block = main_in[l].reshape(src_rows, main_width)
         image_scores = lax.dot_general(
             spread, block[:, :side], NT, preferred_element_type=f32
@@ -319,9 +291,8 @@
                 :, side + (d - 1) * HEAD_DIM:side + d * HEAD_DIM
             ]
 
-    for hop in hops:
-        own_wait(0, hop)
-    own_keys = [own_in[0, :, l].reshape(src_rows, HEAD_DIM) for l in range(layers)]
+    settle(keys_in.at[others], own_recv.at[0])
+    own_keys = [keys_in[:, l].reshape(src_rows, HEAD_DIM) for l in range(layers)]
     mine_now = []
     for l in range(layers):
         image_scores = lax.dot_general(
@@ -350,9 +321,9 @@
     for l in range(layers):
         cache[l, 0, :, lanes_of(0)] = moved[:, l * HEAD_DIM:(l + 1) * HEAD_DIM]
 
-    for l in range(layers):
-        for d in range(1, seq_count):
-            part_copy(l, d).wait_recv()
+    beside = pl.ds(1, seq_count - 1)
+    settle(part_in.at[:, beside], part_sem.at[1])
+    for l in range(layers):
         cells = [mine_now[l]] + [
             tuple(part_in[l, d, :, i * HEAD_DIM:(i + 1) * HEAD_DIM] for i in range(3))
             for d in range(1, seq_count)
@@ -365,26 +336,15 @@
         )
         partial_out[l, :, 2 * HEAD_DIM:] = sum(f * c[2] for f, c in zip(factors, cells))
 
-    for l in range(layers):
-        for hop in hops:
-            main_copy(l, hop).wait_send()
-        for d in range(1, seq_count):
-            part_copy(l, d).wait_send()
-    for hop in hops:
-        place_copy(hop).wait_send()
-        own_copy(0, hop).wait_send()
-    for hop in hops:
-        own_wait(1, hop)
-    for l in range(layers):
-        values_out[:, l * HEAD_DIM:(l + 1) * HEAD_DIM] = own_in[1, :, l].reshape(
-            src_rows, HEAD_DIM
-        )
-    for hop in hops:
-        own_copy(1, hop).wait_send()
+    settle(main_out.at[:, others], main_send.at[0])
+    settle(place_in.at[others], place_sem.at[0])
+    settle(part_out.at[:, beside], part_sem.at[0])
+    settle(own_out.at[:, others], own_send.at[0])
+    settle(values_in.at[others], own_recv.at[1])
 
 
 def finish(
-    dims, cache, put, values, weights, partial, att_out, cache_out, att, last, sem, last_sem
+    dims, cache, put, values, weights, partial, att_out, cache_out, att, last, sem
 ):
     _, seq_count, _ = dims
     layers, _, src_rows, full = cache.shape
@@ -397,35 +357,23 @@
         g = lax.rem(seq + d, seq_count)
         return pl.ds(pl.multiple_of(kvw + g * HEAD_DIM, HEAD_DIM), HEAD_DIM)
 
-    early = []
-    for l in range(layers):
-        early.append(
+    for l in range(layers):
+        pltpu.make_async_copy(
+            cache.at[l, 0, :, pl.ds(0, kvw)], cache_out.at[l, 0, :, pl.ds(0, kvw)], sem.at[0]
+        ).start()
+        for d in range(1, seq_count):
             pltpu.make_async_copy(
-                cache.at[l, 0, :, pl.ds(0, kvw)], cache_out.at[l, 0, :, pl.ds(0, kvw)],
-                sem.at[l, 0],
-            )
-        )
-        for d in range(1, seq_count):
-            early.append(
-                pltpu.make_async_copy(
-                    cache.at[l, 0, :, lanes_of(d)], cache_out.at[l, 0, :, lanes_of(d)],
-                    sem.at[l, d],
-                )
-            )
-    for copy in early:
-        copy.start()
-    late = []
+                cache.at[l, 0, :, lanes_of(d)], cache_out.at[l, 0, :, lanes_of(d)], sem.at[0]
+            ).start()
+    own = [values[:, l].reshape(src_rows, HEAD_DIM) for l in range(layers)]
     both = jnp.concatenate([put[...], weights[...].astype(bf16)], axis=0)
-    moved = jnp.dot(both, values[...], preferred_element_type=f32)
+    moved = jnp.dot(both, jnp.concatenate(own, axis=1), preferred_element_type=f32)
     for l in range(layers):
         at = slice(l * HEAD_DIM, (l + 1) * HEAD_DIM)
         last[l] = moved[:src_rows, at].astype(bf16)
-        late.append(
-            pltpu.make_async_copy(
-                last.at[l], cache_out.at[l, 0, :, lanes_of(0)], last_sem.at[l]
-            )
-        )
-        late[-1].start()
+        pltpu.make_async_copy(
+            last.at[l], cache_out.at[l, 0, :, lanes_of(0)], sem.at[0]
+        ).start()
     lines = []
     for l in range(layers):
         value = moved[
@@ -436,10 +384,10 @@
         result = (summed + factor * value) / partial[l, :, 2 * HEAD_DIM:]
         lines.append(jnp.concatenate([result[h:h + 1] for h in range(group)], axis=1))
     att[...] = jnp.concatenate(lines, axis=0).astype(bf16)
-    late.append(pltpu.make_async_copy(att, att_out, last_sem.at[layers]))
-    late[-1].start()
-    for copy in early + late:
-        copy.wait()
+    att_copy = pltpu.make_async_copy(att, att_out, sem.at[1])
+    att_copy.start()
+    pltpu.make_async_copy(cache, cache_out, sem.at[0]).wait()
+    att_copy.wait()
 
 
 def body(dims, query, text_cache, text_len, image_rows, patch_map, image_places):
@@ -466,7 +414,7 @@
         out_shape=(
             pltpu.VMEM(cache_shape.shape, bf16),
             pltpu.VMEM((src_rows, src_rows), bf16),
-            pltpu.VMEM((src_rows, layers * HEAD_DIM), bf16),
+            pltpu.VMEM((groups, layers, per, HEAD_DIM), bf16),
             pltpu.VMEM((layers * PAD, src_rows), f32),
             pltpu.VMEM((layers, PAD, 3 * HEAD_DIM), f32),
         ),
@@ -482,16 +430,15 @@
             pltpu.VMEM((layers, groups, per, main_width), bf16),
             pltpu.VMEM((layers, groups, per, main_width), bf16),
             pltpu.VMEM((2, groups, layers, per, HEAD_DIM), bf16),
-            pltpu.VMEM((2, groups, layers, per, HEAD_DIM), bf16),
+            pltpu.VMEM((groups, layers, per, HEAD_DIM), bf16),
             pltpu.VMEM((1, src_rows), i32),
             pltpu.VMEM((groups, 1, src_rows), i32),
             pltpu.VMEM((layers, rows_padded, HEAD_DIM), f32),
             pltpu.VMEM((layers, rows_padded, text_dev), f32),
             pltpu.VMEM((layers, seq_count, PAD, 3 * HEAD_DIM), f32),
             pltpu.VMEM((layers, seq_count, PAD, 3 * HEAD_DIM), f32),
-            dma((4,)), dma((layers,)), dma((layers,)),
-            dma((layers, groups)), dma((layers, groups)), dma((2, groups)), dma((2, groups)),
-            dma((groups,)), dma((groups,)), dma((layers, seq_count)), dma((layers, seq_count)),
+            dma((4,)), dma((2,)), dma((1,)), dma((1,)), dma((layers,)), dma((1,)), dma((2,)),
+            dma((2,)), dma((2,)),
         ],
         compiler_params=pltpu.CompilerParams(
             collective_id=0, has_side_effects=True, vmem_limit_bytes=32 * 1024 * 1024
@@ -509,7 +456,7 @@
         scratch_shapes=[
             pltpu.VMEM(att_shape.shape, bf16),
             pltpu.VMEM((layers, src_rows, HEAD_DIM), bf16),
-            dma((layers, seq_count)), dma((layers + 1,)),
+            dma((2,)),
         ],
     )(*(in_vmem(x) for x in state))
     return attended.reshape(layers, 1, query_width // seq_count), cache

time: 54.5 us -> 52.9 us (0.971)
  Pallas kernels: 53.1 us -> 51.5 us
    pallas_call x1, Pallas kernels: 51.6 us -> 50.1 us  [body(): pl.pallas_call(functools.partial(exchange, dims), out_shape=(pltpu.VMEM(c...]
where the time goes in v2:
time: 52.9 us; the launch traced here: 52.7 us
  Pallas kernels  51.5 us (97%)
  between operations  1.28 us (2%)
    pallas_call x1, Pallas kernels, body(): pl.pallas_call(functools.partial(exchange, dims), out_shape=(pltpu.VMEM(c...  50.1 us
    pallas_call x1, Pallas kernels, body(): pl.pallas_call(functools.partial(finish, dims), out_shape=(att_shape, cac...  1.34 us

profile of v2, /device:TPU:9, one launch (start us, length us, event | category | flops | bytes accessed | tf_op | source)
XLA Modules:
  0.0 52.7 jit_solution(16516297527327687466)
XLA Ops:
  1.3 50.1 %shard_map.77 = (bf16[4,1,256,1024]{3,2,1,0:T(8,128)(2,1)S(1)}, bf16[256,256]{1,0:T(8,128)(2,1)S(1)}, bf16[8,4,32,128]{3,2,1,0:T(8,128)(2,1)S(1)}, f32[32,256]{1,0:T(8,128)S(1)}, f32[4,8,384]{2,1,0:T(8,128)S(1)}) custom-call(bf16[4,3584]{1,0:T(4,128)(2,1)} %bitcast.4, s32[1]{0:T(128)S(6)} %copy.8.len_hbm, s32[1,256]{1,0:T(1,128)} %bitcast.5, ...), custom_call_target="tpu_custom_call" | custom-call | tf_op jit(solution)/shard_map/pallas_call | solution.py:412
  51.4 1.3 %shard_map.78 = (bf16[4,896]{1,0:T(4,128)(2,1)}, bf16[4,1,256,1024]{3,2,1,0:T(8,128)(2,1)}) custom-call(bf16[4,1,256,1024]{3,2,1,0:T(8,128)(2,1)S(1)} %get-tuple-element.9.cache, bf16[256,256]{1,0:T(8,128)(2,1)S(1)} %get-tuple-element.10.put, bf16[8,4,32,128]{3,2,1,0:T(8,128)(2,1)S(1)} %get-tuple-element.11.values, f32[32,256]{1,0:T(8,128)S(1)} %get-tuple-element.12.weights, ...), custom_call_target="tpu_custom_call" | custom-call | tf_op jit(solution)/shard_map/pallas_call | solution.py:451

commit v3 on v2

--- a/solution.py
+++ b/solution.py
@@ -33,6 +33,7 @@
     query, length, maps, places, rows, text, main_out, main_in, own_out, keys_in, place_out, place_in,
     heads, scores, part_out, part_in,
     small_sem, rows_sem, text_sem, main_send, main_recv, own_send, own_recv, place_sem, part_sem,
+    info,
 ):
     patch_count, seq_count, req_count = dims
     layers, src_rows, full = rows.shape
@@ -49,9 +50,12 @@
     me = patch * req_count + req
     near = near_hops(patch_count, req_count)
     far = [far_hops(patch_count, req_count, k) for k in range(half)]
-    hops = near + [hop for wave in far for hop in wave]
+    early = near if half <= 2 else [hop for hop in near if hop[1] == 0]
+    late = [hop for hop in near if hop not in early]
+    ahead = min(2, layers)
     f32, bf16 = jnp.float32, jnp.bfloat16
     upper = patch // half
+    inner = jnp.logical_or(patch == half - 1, patch == half)
 
     def partner(hop):
         kind, i, c = hop
@@ -79,12 +83,37 @@
     small[0].start()
     first_rows.start()
     barrier = pltpu.get_barrier_semaphore()
-    for hop in hops:
-        p, r = partner(hop)
-        pl.semaphore_signal(barrier, inc=1, device_id=(p, seq, r), device_id_type=MESH)
-    for d in range(1, seq_count):
-        s = lax.rem(seq + d, seq_count)
-        pl.semaphore_signal(barrier, inc=1, device_id=(patch, s, req), device_id_type=MESH)
+
+    def tell(sem, p, s, r):
+        pl.semaphore_signal(sem, inc=1, device_id=(p, s, r), device_id_type=MESH)
+
+    above, below = patch < patch_count - 1, patch > 0
+
+    @pl.when(above)
+    def _():
+        for c in range(req_count):
+            tell(barrier, patch + 1, seq, lax.rem(req + c, req_count))
+
+    @pl.when(below)
+    def _():
+        for c in range(req_count):
+            tell(barrier, patch - 1, seq, lax.rem(req + c, req_count))
+
+    for c in range(1, req_count):
+        tell(barrier, patch, seq, lax.rem(req + c, req_count))
+
+    @pl.when(patch == 0)
+    def _():
+        for d in range(1, seq_count):
+            tell(barrier, patch, lax.rem(seq + d, seq_count), req)
+
+    has_above = 1 - patch // (patch_count - 1)
+    has_below = 1 - (patch_count - 1 - patch) // (patch_count - 1)
+    arrivals = (
+        req_count - 1 + req_count * (has_above + has_below)
+        + (seq_count - 1) * (1 - has_below)
+    )
+
     for copy in small[1:]:
         copy.start()
 
@@ -150,12 +179,25 @@
         moved = jnp.dot(pick, turned, preferred_element_type=f32).astype(bf16)
         main_out[l] = moved.reshape(groups, per, main_width)
         if l == 0:
-            pl.semaphore_wait(barrier, len(hops) + seq_count - 1)
-        for hop in near:
+            pl.semaphore_wait(barrier, arrivals)
+
+            @pl.when(jnp.logical_and(patch == 1, above))
+            def _():
+                tell(info.at[1], patch + 1, seq, req)
+
+            @pl.when(jnp.logical_and(patch == patch_count - 2, below))
+            def _():
+                tell(info.at[0], patch - 1, seq, req)
+
+        for hop in early:
             main_copy(l, hop).start()
-        for wave in far[:-1]:
-            for hop in wave:
-                main_copy(l, hop).start()
+        if l < ahead:
+
+            @pl.when(inner)
+            def _():
+                for hop in far[-1]:
+                    main_copy(l, hop).start()
+
         if l == 0:
             small[1].wait()
             local = (places[...] - seq * src_rows).astype(f32).astype(bf16)
@@ -165,7 +207,7 @@
             )
             place_out[...] = place_sorted[0:1].astype(jnp.int32)
             place_in[me] = place_sorted[0:1].astype(jnp.int32)
-            for hop in hops:
+            for hop in early:
                 place_copy(hop).start()
     for l in range(layers):
         turned = jnp.concatenate([rows[l, :, lanes_of(0)], rows[l, :, lanes_of(0, kvw)]], axis=1)
@@ -173,9 +215,46 @@
         own_out[0, :, l] = moved[:, :HEAD_DIM].reshape(groups, per, HEAD_DIM)
         own_out[1, :, l] = moved[:, HEAD_DIM:].reshape(groups, per, HEAD_DIM)
     for i in range(2):
-        for hop in near:
+        for hop in early:
             own_copy(i, hop).start()
-    for l in range(layers):
+
+    @pl.when(patch < patch_count - 2)
+    def _():
+        pl.semaphore_wait(info.at[0], 1)
+
+    @pl.when(jnp.logical_and(patch < patch_count - 2, below))
+    def _():
+        tell(info.at[0], patch - 1, seq, req)
+
+    @pl.when(patch > 1)
+    def _():
+        pl.semaphore_wait(info.at[1], 1)
+
+    @pl.when(jnp.logical_and(patch > 1, above))
+    def _():
+        tell(info.at[1], patch + 1, seq, req)
+
+    for hop in late:
+        place_copy(hop).start()
+        for l in range(layers):
+            main_copy(l, hop).start()
+        for i in range(2):
+            own_copy(i, hop).start()
+    for wave in far:
+        for hop in wave:
+            place_copy(hop).start()
+    for l in range(layers):
+        for wave in far[:-1]:
+            for hop in wave:
+                main_copy(l, hop).start()
+
+    @pl.when(jnp.logical_not(inner))
+    def _():
+        for l in range(ahead):
+            for hop in far[-1]:
+                main_copy(l, hop).start()
+
+    for l in range(ahead, layers):
         for hop in far[-1]:
             main_copy(l, hop).start()
     for wave in far:
@@ -239,6 +318,18 @@
     place = jnp.sum(jnp.where(source == owner, lanes, 0.0), axis=0, keepdims=True)
     put = (row_i == place.astype(jnp.int32)).astype(f32).astype(bf16)
     put_out[...] = put
+
+    @pl.when(patch == 0)
+    def _():
+        for d in range(1, seq_count):
+            tell(info.at[2], patch, lax.rem(seq + d, seq_count), req)
+        pl.semaphore_wait(info.at[2], seq_count - 1)
+        for p in range(1, patch_count):
+            tell(info.at[3], p, seq, req)
+
+    @pl.when(below)
+    def _():
+        pl.semaphore_wait(info.at[3], 1)
 
     zeros = jnp.zeros((PAD, HEAD_DIM), f32)
     for l in range(layers):
@@ -438,7 +529,7 @@
             pltpu.VMEM((layers, seq_count, PAD, 3 * HEAD_DIM), f32),
             pltpu.VMEM((layers, seq_count, PAD, 3 * HEAD_DIM), f32),
             dma((4,)), dma((2,)), dma((1,)), dma((1,)), dma((layers,)), dma((1,)), dma((2,)),
-            dma((2,)), dma((2,)),
+            dma((2,)), dma((2,)), pltpu.SemaphoreType.REGULAR((4,)),
         ],
         compiler_params=pltpu.CompilerParams(
             collective_id=0, has_side_effects=True, vmem_limit_bytes=32 * 1024 * 1024

time: 52.9 us -> 52.8 us (level)
  no operation moved by 1% of the time
where the time goes in v3:
time: 52.8 us; the launch traced here: 52.6 us
  Pallas kernels  51.3 us (97%)
  between operations  1.28 us (2%)
    pallas_call x1, Pallas kernels, body(): pl.pallas_call(functools.partial(exchange, dims), out_shape=(pltpu.VMEM(c...  50 us
    pallas_call x1, Pallas kernels, body(): pl.pallas_call(functools.partial(finish, dims), out_shape=(att_shape, cac...  1.34 us

profile of v3, /device:TPU:9, one launch (start us, length us, event | category | flops | bytes accessed | tf_op | source)
XLA Modules:
  0.0 52.6 jit_solution(18056843378474630216)
XLA Ops:
  1.3 50.0 %shard_map.77 = (bf16[4,1,256,1024]{3,2,1,0:T(8,128)(2,1)S(1)}, bf16[256,256]{1,0:T(8,128)(2,1)S(1)}, bf16[8,4,32,128]{3,2,1,0:T(8,128)(2,1)S(1)}, f32[32,256]{1,0:T(8,128)S(1)}, f32[4,8,384]{2,1,0:T(8,128)S(1)}) custom-call(bf16[4,3584]{1,0:T(4,128)(2,1)} %bitcast.4, s32[1]{0:T(128)S(6)} %copy.8.len_hbm, s32[1,256]{1,0:T(1,128)} %bitcast.5, ...), custom_call_target="tpu_custom_call" | custom-call | tf_op jit(solution)/shard_map/pallas_call | solution.py:503
  51.2 1.3 %shard_map.78 = (bf16[4,896]{1,0:T(4,128)(2,1)}, bf16[4,1,256,1024]{3,2,1,0:T(8,128)(2,1)}) custom-call(bf16[4,1,256,1024]{3,2,1,0:T(8,128)(2,1)S(1)} %get-tuple-element.9.cache, bf16[256,256]{1,0:T(8,128)(2,1)S(1)} %get-tuple-element.10.put, bf16[8,4,32,128]{3,2,1,0:T(8,128)(2,1)S(1)} %get-tuple-element.11.values, f32[32,256]{1,0:T(8,128)S(1)} %get-tuple-element.12.weights, ...), custom_call_target="tpu_custom_call" | custom-call | tf_op jit(solution)/shard_map/pallas_call | solution.py:542

commit v4 on v3

--- a/solution.py
+++ b/solution.py
@@ -16,14 +16,13 @@
 NT = (((1,), (1,)), ((), ()))
 
 
-def near_hops(patch_count, req_count):
+def all_hops(patch_count, req_count):
     half = patch_count // 2
-    beside = [("near", i, c) for i in range(1, half) for c in range(req_count)]
-    return beside + [("near", 0, c) for c in range(1, req_count)]
-
-
-def far_hops(patch_count, req_count, k):
-    return [("far", k, c) for c in range(req_count)]
+    cores = range(req_count)
+    mates = [("mate", 0, c) for c in cores if c]
+    near = [("near", i, c) for i in range(1, half) for c in cores]
+    far = [[("far", k, c) for c in cores] for k in range(half)]
+    return mates, near, far
 
 
 def exchange(
@@ -48,10 +47,9 @@
     scale = 1.0 / math.sqrt(HEAD_DIM)
     patch, seq, req = (lax.axis_index(a) for a in ("patch", "seq", "req"))
     me = patch * req_count + req
-    near = near_hops(patch_count, req_count)
-    far = [far_hops(patch_count, req_count, k) for k in range(half)]
-    early = near if half <= 2 else [hop for hop in near if hop[1] == 0]
-    late = [hop for hop in near if hop not in early]
+    mates, near, far = all_hops(patch_count, req_count)
+    beside = near if half == 2 else []
+    late = [hop for hop in near if hop not in beside]
     ahead = min(2, layers)
     f32, bf16 = jnp.float32, jnp.bfloat16
     upper = patch // half
@@ -59,16 +57,22 @@
 
     def partner(hop):
         kind, i, c = hop
-        r = lax.rem(req + c, req_count)
+        r = req_count - 1 - c
+        if kind == "mate":
+            return patch, lax.rem(req + c, req_count)
         if kind == "near":
             return upper * half + lax.rem(lax.rem(patch, half) + i, half), r
         return (1 - upper) * (patch_count - 1 - i) + upper * i, r
 
     others = pl.ds(0, groups - 1)
     own_in = (keys_in, values_in)
-    first_rows = pltpu.make_async_copy(rows_hbm.at[0], rows.at[0], rows_sem.at[0])
+    halves = (pl.ds(0, kvw), pl.ds(kvw, kvw))
+    first_rows = [
+        pltpu.make_async_copy(rows_hbm.at[0, :, at], rows.at[0, :, at], rows_sem.at[1 + i])
+        for i, at in enumerate(halves)
+    ]
     later = pl.ds(1, layers - 1)
-    later_rows = pltpu.make_async_copy(rows_hbm.at[later], rows.at[later], rows_sem.at[1])
+    later_rows = pltpu.make_async_copy(rows_hbm.at[later], rows.at[later], rows_sem.at[0])
     text_copy = pltpu.make_async_copy(text_hbm.at[:, 0], text, text_sem.at[0])
 
     def settle(ref, sem):
@@ -81,7 +85,8 @@
         pltpu.make_async_copy(len_hbm, length, small_sem.at[3]),
     ]
     small[0].start()
-    first_rows.start()
+    for copy in first_rows:
+        copy.start()
     barrier = pltpu.get_barrier_semaphore()
 
     def tell(sem, p, s, r):
@@ -94,7 +99,7 @@
         for c in range(req_count):
             tell(barrier, patch + 1, seq, lax.rem(req + c, req_count))
 
-    @pl.when(below)
+    @pl.when(jnp.logical_and(below, patch <= half))
     def _():
         for c in range(req_count):
             tell(barrier, patch - 1, seq, lax.rem(req + c, req_count))
@@ -107,15 +112,20 @@
         for d in range(1, seq_count):
             tell(barrier, patch, lax.rem(seq + d, seq_count), req)
 
-    has_above = 1 - patch // (patch_count - 1)
     has_below = 1 - (patch_count - 1 - patch) // (patch_count - 1)
     arrivals = (
-        req_count - 1 + req_count * (has_above + has_below)
-        + (seq_count - 1) * (1 - has_below)
+        req_count - 1 + req_count * (has_below + 1 - upper) + (seq_count - 1) * (1 - has_below)
     )
+    answers = jnp.logical_and(patch == patch_count - 1, patch > half)
 
     for copy in small[1:]:
         copy.start()
+
+    @pl.when(answers)
+    def _():
+        pl.semaphore_wait(barrier, arrivals)
+        tell(info.at[0], patch - 1, seq, req)
+
 
     def lanes_of(d, base=0):
         g = lax.rem(seq + d, seq_count)
@@ -141,10 +151,10 @@
             device_id=(p, seq, r), device_id_type=MESH,
         )
 
-    def main_copy(l, hop):
+    def main_copy(l, hop, at=pl.ds(0, main_width)):
         p, r = partner(hop)
         return pltpu.make_async_remote_copy(
-            src_ref=main_out.at[l, p * req_count + r], dst_ref=main_in.at[l, me],
+            src_ref=main_out.at[l, p * req_count + r, :, at], dst_ref=main_in.at[l, me, :, at],
             send_sem=main_send.at[0], recv_sem=main_recv.at[l],
             device_id=(p, seq, r), device_id_type=MESH,
         )
@@ -165,39 +175,55 @@
             device_id=(patch, s, req), device_id_type=MESH,
         )
 
+    def sort(l, base):
+        turned = jnp.concatenate(
+            [rows[l, :, lanes_of(d, base)] for d in range(1, seq_count)], axis=1
+        )
+        moved = jnp.dot(pick, turned, preferred_element_type=f32).astype(bf16)
+        at = slice(0, side) if base == 0 else slice(side, main_width)
+        main_out[l, :, :, at] = moved.reshape(groups, per, side)
+
+    def send_first(l, at):
+        for hop in mates:
+            main_copy(l, hop, at).start()
+
+        @pl.when(patch != half)
+        def _():
+            for hop in beside:
+                main_copy(l, hop, at).start()
+
+        if l < ahead:
+
+            @pl.when(inner)
+            def _():
+                for hop in far[-1]:
+                    main_copy(l, hop, at).start()
+
     for l in range(layers):
         if l == 0:
-            first_rows.wait()
+            first_rows[0].wait()
+            sort(l, 0)
+
+            @pl.when(jnp.logical_not(answers))
+            def _():
+                pl.semaphore_wait(barrier, arrivals)
+
+            send_first(l, pl.ds(0, side))
+            first_rows[1].wait()
             later_rows.start()
-        if l == 1:
-            later_rows.wait()
-        turned = jnp.concatenate(
-            [rows[l, :, lanes_of(d)] for d in range(1, seq_count)]
-            + [rows[l, :, lanes_of(d, kvw)] for d in range(1, seq_count)],
-            axis=1,
-        )
-        moved = jnp.dot(pick, turned, preferred_element_type=f32).astype(bf16)
-        main_out[l] = moved.reshape(groups, per, main_width)
-        if l == 0:
-            pl.semaphore_wait(barrier, arrivals)
+            sort(l, kvw)
+            send_first(l, pl.ds(side, side))
 
             @pl.when(jnp.logical_and(patch == 1, above))
             def _():
                 tell(info.at[1], patch + 1, seq, req)
 
-            @pl.when(jnp.logical_and(patch == patch_count - 2, below))
-            def _():
-                tell(info.at[0], patch - 1, seq, req)
-
-        for hop in early:
-            main_copy(l, hop).start()
-        if l < ahead:
-
-            @pl.when(inner)
-            def _():
-                for hop in far[-1]:
-                    main_copy(l, hop).start()
-
+        else:
+            if l == 1:
+                later_rows.wait()
+            sort(l, 0)
+            sort(l, kvw)
+            send_first(l, pl.ds(0, main_width))
         if l == 0:
             small[1].wait()
             local = (places[...] - seq * src_rows).astype(f32).astype(bf16)
@@ -207,22 +233,31 @@
             )
             place_out[...] = place_sorted[0:1].astype(jnp.int32)
             place_in[me] = place_sorted[0:1].astype(jnp.int32)
-            for hop in early:
+            for hop in mates:
                 place_copy(hop).start()
     for l in range(layers):
         turned = jnp.concatenate([rows[l, :, lanes_of(0)], rows[l, :, lanes_of(0, kvw)]], axis=1)
         moved = jnp.dot(pick, turned, preferred_element_type=f32).astype(bf16)
         own_out[0, :, l] = moved[:, :HEAD_DIM].reshape(groups, per, HEAD_DIM)
         own_out[1, :, l] = moved[:, HEAD_DIM:].reshape(groups, per, HEAD_DIM)
+    def own_near():
+        for i in range(2):
+            for hop in beside:
+                own_copy(i, hop).start()
+
     for i in range(2):
-        for hop in early:
+        for hop in mates:
             own_copy(i, hop).start()
-
-    @pl.when(patch < patch_count - 2)
+    pl.when(patch != half)(own_near)
+    listens = jnp.logical_or(
+        patch < patch_count - 2, jnp.logical_and(patch >= half, above)
+    )
+
+    @pl.when(listens)
     def _():
         pl.semaphore_wait(info.at[0], 1)
 
-    @pl.when(jnp.logical_and(patch < patch_count - 2, below))
+    @pl.when(jnp.logical_and(listens, below))
     def _():
         tell(info.at[0], patch - 1, seq, req)
 
@@ -234,6 +269,15 @@
     def _():
         tell(info.at[1], patch + 1, seq, req)
 
+    @pl.when(patch == half)
+    def _():
+        for l in range(layers):
+            for hop in beside:
+                main_copy(l, hop).start()
+        own_near()
+
+    for hop in beside:
+        place_copy(hop).start()
     for hop in late:
         place_copy(hop).start()
         for l in range(layers):
@@ -412,8 +456,8 @@
     for l in range(layers):
         cache[l, 0, :, lanes_of(0)] = moved[:, l * HEAD_DIM:(l + 1) * HEAD_DIM]
 
-    beside = pl.ds(1, seq_count - 1)
-    settle(part_in.at[:, beside], part_sem.at[1])
+    bands = pl.ds(1, seq_count - 1)
+    settle(part_in.at[:, bands], part_sem.at[1])
     for l in range(layers):
         cells = [mine_now[l]] + [
             tuple(part_in[l, d, :, i * HEAD_DIM:(i + 1) * HEAD_DIM] for i in range(3))
@@ -429,7 +473,7 @@
 
     settle(main_out.at[:, others], main_send.at[0])
     settle(place_in.at[others], place_sem.at[0])
-    settle(part_out.at[:, beside], part_sem.at[0])
+    settle(part_out.at[:, bands], part_sem.at[0])
     settle(own_out.at[:, others], own_send.at[0])
     settle(values_in.at[others], own_recv.at[1])
 
@@ -528,7 +572,7 @@
             pltpu.VMEM((layers, rows_padded, text_dev), f32),
             pltpu.VMEM((layers, seq_count, PAD, 3 * HEAD_DIM), f32),
             pltpu.VMEM((layers, seq_count, PAD, 3 * HEAD_DIM), f32),
-            dma((4,)), dma((2,)), dma((1,)), dma((1,)), dma((layers,)), dma((1,)), dma((2,)),
+            dma((4,)), dma((3,)), dma((1,)), dma((1,)), dma((layers,)), dma((1,)), dma((2,)),
             dma((2,)), dma((2,)), pltpu.SemaphoreType.REGULAR((4,)),
         ],
         compiler_params=pltpu.CompilerParams(

time: 52.8 us -> 51.8 us (0.981)
  Pallas kernels: 51.3 us -> 50 us
    pallas_call x1, Pallas kernels: 50 us -> 48.6 us  [body(): pl.pallas_call(functools.partial(exchange, dims), out_shape=(pltpu.VMEM(c...]
where the time goes in v4:
time: 51.8 us; the launch traced here: 51.2 us
  Pallas kernels  50 us (97%)
  between operations  1.28 us (2%)
    pallas_call x1, Pallas kernels, body(): pl.pallas_call(functools.partial(exchange, dims), out_shape=(pltpu.VMEM(c...  48.6 us
    pallas_call x1, Pallas kernels, body(): pl.pallas_call(functools.partial(finish, dims), out_shape=(att_shape, cac...  1.34 us

profile of v4, /device:TPU:9, one launch (start us, length us, event | category | flops | bytes accessed | tf_op | source)
XLA Modules:
  0.0 51.2 jit_solution(957491503087610244)
XLA Ops:
  1.3 48.6 %shard_map.77 = (bf16[4,1,256,1024]{3,2,1,0:T(8,128)(2,1)S(1)}, bf16[256,256]{1,0:T(8,128)(2,1)S(1)}, bf16[8,4,32,128]{3,2,1,0:T(8,128)(2,1)S(1)}, f32[32,256]{1,0:T(8,128)S(1)}, f32[4,8,384]{2,1,0:T(8,128)S(1)}) custom-call(bf16[4,3584]{1,0:T(4,128)(2,1)} %bitcast.4, s32[1]{0:T(128)S(6)} %copy.8.len_hbm, s32[1,256]{1,0:T(1,128)} %bitcast.5, ...), custom_call_target="tpu_custom_call" | custom-call | tf_op jit(solution)/shard_map/pallas_call | solution.py:547
  49.9 1.3 %shard_map.78 = (bf16[4,896]{1,0:T(4,128)(2,1)}, bf16[4,1,256,1024]{3,2,1,0:T(8,128)(2,1)}) custom-call(bf16[4,1,256,1024]{3,2,1,0:T(8,128)(2,1)S(1)} %get-tuple-element.9.cache, bf16[256,256]{1,0:T(8,128)(2,1)S(1)} %get-tuple-element.10.put, bf16[8,4,32,128]{3,2,1,0:T(8,128)(2,1)S(1)} %get-tuple-element.11.values, f32[32,256]{1,0:T(8,128)S(1)} %get-tuple-element.12.weights, ...), custom_call_target="tpu_custom_call" | custom-call | tf_op jit(solution)/shard_map/pallas_call | solution.py:586

commit v5 on v4

--- a/solution.py
+++ b/solution.py
@@ -31,7 +31,7 @@
     cache, put_out, values_in, weights_out, partial_out,
     query, length, maps, places, rows, text, main_out, main_in, own_out, keys_in, place_out, place_in,
     heads, scores, part_out, part_in,
-    small_sem, rows_sem, text_sem, main_send, main_recv, own_send, own_recv, place_sem, part_sem,
+    small_sem, load_sem, main_send, main_recv, own_send, own_recv, place_sem, part_sem,
     info,
 ):
     patch_count, seq_count, req_count = dims
@@ -57,9 +57,9 @@
 
     def partner(hop):
         kind, i, c = hop
-        r = req_count - 1 - c
         if kind == "mate":
             return patch, lax.rem(req + c, req_count)
+        r = req_count - 1 - c if kind == "near" or i == half - 1 else c
         if kind == "near":
             return upper * half + lax.rem(lax.rem(patch, half) + i, half), r
         return (1 - upper) * (patch_count - 1 - i) + upper * i, r
@@ -68,21 +68,22 @@
     own_in = (keys_in, values_in)
     halves = (pl.ds(0, kvw), pl.ds(kvw, kvw))
     first_rows = [
-        pltpu.make_async_copy(rows_hbm.at[0, :, at], rows.at[0, :, at], rows_sem.at[1 + i])
+        pltpu.make_async_copy(rows_hbm.at[0, :, at], rows.at[0, :, at], load_sem.at[i])
         for i, at in enumerate(halves)
     ]
-    later = pl.ds(1, layers - 1)
-    later_rows = pltpu.make_async_copy(rows_hbm.at[later], rows.at[later], rows_sem.at[0])
-    text_copy = pltpu.make_async_copy(text_hbm.at[:, 0], text, text_sem.at[0])
+    second_rows = pltpu.make_async_copy(rows_hbm.at[1], rows.at[1], load_sem.at[2])
+    rest = pl.ds(2, layers - 2)
+    rest_rows = pltpu.make_async_copy(rows_hbm.at[rest], rows.at[rest], load_sem.at[3])
+    text_copy = pltpu.make_async_copy(text_hbm.at[:, 0], text, load_sem.at[0])
 
     def settle(ref, sem):
         pltpu.make_async_copy(ref, ref, sem).wait()
 
     small = [
         pltpu.make_async_copy(map_hbm, maps, small_sem.at[0]),
-        pltpu.make_async_copy(place_hbm, places, small_sem.at[1]),
-        pltpu.make_async_copy(query_hbm, query, small_sem.at[2]),
-        pltpu.make_async_copy(len_hbm, length, small_sem.at[3]),
+        pltpu.make_async_copy(place_hbm, places, small_sem.at[0]),
+        pltpu.make_async_copy(query_hbm, query, small_sem.at[0]),
+        pltpu.make_async_copy(len_hbm, length, small_sem.at[0]),
     ]
     small[0].start()
     for copy in first_rows:
@@ -94,15 +95,15 @@
 
     above, below = patch < patch_count - 1, patch > 0
 
+    @pl.when(jnp.logical_and(below, patch <= half))
+    def _():
+        for c in range(req_count):
+            tell(barrier, patch - 1, seq, lax.rem(req + c, req_count))
+
     @pl.when(above)
     def _():
         for c in range(req_count):
             tell(barrier, patch + 1, seq, lax.rem(req + c, req_count))
-
-    @pl.when(jnp.logical_and(below, patch <= half))
-    def _():
-        for c in range(req_count):
-            tell(barrier, patch - 1, seq, lax.rem(req + c, req_count))
 
     for c in range(1, req_count):
         tell(barrier, patch, seq, lax.rem(req + c, req_count))
@@ -117,9 +118,6 @@
         req_count - 1 + req_count * (has_below + 1 - upper) + (seq_count - 1) * (1 - has_below)
     )
     answers = jnp.logical_and(patch == patch_count - 1, patch > half)
-
-    for copy in small[1:]:
-        copy.start()
 
     @pl.when(answers)
     def _():
@@ -136,6 +134,7 @@
     col_i = lax.broadcasted_iota(jnp.int32, (src_rows, src_rows), 1)
     before = (row_i < col_i).astype(f32).astype(bf16)
     small[0].wait()
+    small[1].start()
     mine = maps[...] == owner
     rank = jnp.dot(mine.astype(f32).astype(bf16), before, preferred_element_type=f32)
     slot = jnp.sum(
@@ -202,6 +201,8 @@
     for l in range(layers):
         if l == 0:
             first_rows[0].wait()
+            second_rows.start()
+            rest_rows.start()
             sort(l, 0)
 
             @pl.when(jnp.logical_not(answers))
@@ -210,7 +211,6 @@
 
             send_first(l, pl.ds(0, side))
             first_rows[1].wait()
-            later_rows.start()
             sort(l, kvw)
             send_first(l, pl.ds(side, side))
 
@@ -220,12 +220,15 @@
 
         else:
             if l == 1:
-                later_rows.wait()
+                second_rows.wait()
+            if l == 2:
+                rest_rows.wait()
             sort(l, 0)
             sort(l, kvw)
             send_first(l, pl.ds(0, main_width))
         if l == 0:
             small[1].wait()
+            small[2].start()
             local = (places[...] - seq * src_rows).astype(f32).astype(bf16)
             place_sorted = lax.dot_general(
                 jnp.broadcast_to(local, (PAD, src_rows)), pick, NT,
@@ -235,6 +238,12 @@
             place_in[me] = place_sorted[0:1].astype(jnp.int32)
             for hop in mates:
                 place_copy(hop).start()
+
+            @pl.when(patch != half)
+            def _():
+                for hop in beside:
+                    place_copy(hop).start()
+
     for l in range(layers):
         turned = jnp.concatenate([rows[l, :, lanes_of(0)], rows[l, :, lanes_of(0, kvw)]], axis=1)
         moved = jnp.dot(pick, turned, preferred_element_type=f32).astype(bf16)
@@ -269,15 +278,20 @@
     def _():
         tell(info.at[1], patch + 1, seq, req)
 
+    @pl.when(patch == 0)
+    def _():
+        for d in range(1, seq_count):
+            tell(info.at[2], patch, lax.rem(seq + d, seq_count), req)
+
     @pl.when(patch == half)
     def _():
+        for hop in beside:
+            place_copy(hop).start()
         for l in range(layers):
             for hop in beside:
                 main_copy(l, hop).start()
         own_near()
 
-    for hop in beside:
-        place_copy(hop).start()
     for hop in late:
         place_copy(hop).start()
         for l in range(layers):
@@ -312,6 +326,7 @@
         own_in[i][me] = own_out[i, me]
 
     small[2].wait()
+    small[3].start()
     lines = query[...].astype(f32)
     for l in range(layers):
         for g in range(KV_HEADS):
@@ -352,6 +367,16 @@
         ) * scale
         scores[l] = jnp.where(used, raw, -jnp.inf)
 
+    @pl.when(patch == 0)
+    def _():
+        pl.semaphore_wait(info.at[2], seq_count - 1)
+        for p in range(1, patch_count):
+            tell(info.at[2], p, seq, req)
+
+    @pl.when(below)
+    def _():
+        pl.semaphore_wait(info.at[2], 1)
+
     settle(place_in.at[others], place_sem.at[1])
     wanted = (row_i == me * per + lax.rem(col_i, per)).astype(f32).astype(bf16)
     lanes = jnp.dot(
@@ -362,18 +387,6 @@
     place = jnp.sum(jnp.where(source == owner, lanes, 0.0), axis=0, keepdims=True)
     put = (row_i == place.astype(jnp.int32)).astype(f32).astype(bf16)
     put_out[...] = put
-
-    @pl.when(patch == 0)
-    def _():
-        for d in range(1, seq_count):
-            tell(info.at[2], patch, lax.rem(seq + d, seq_count), req)
-        pl.semaphore_wait(info.at[2], seq_count - 1)
-        for p in range(1, patch_count):
-            tell(info.at[3], p, seq, req)
-
-    @pl.when(below)
-    def _():
-        pl.semaphore_wait(info.at[3], 1)
 
     zeros = jnp.zeros((PAD, HEAD_DIM), f32)
     for l in range(layers):
@@ -392,23 +405,18 @@
         image_scores = lax.dot_general(
             spread, block[:, :side], NT, preferred_element_type=f32
         ) * scale
-        text_scores = scores[l, PAD:, :]
-        top = jnp.maximum(
-            jnp.max(text_scores, axis=1, keepdims=True),
-            jnp.max(image_scores, axis=1, keepdims=True),
-        )
-        text_w = jnp.exp(text_scores - top)
-        image_w = jnp.exp(image_scores - top)
-        total = jnp.sum(text_w, axis=1, keepdims=True) + jnp.sum(
-            image_w, axis=1, keepdims=True
-        )
+        both = jnp.concatenate([scores[l, PAD:, :], image_scores], axis=1)
+        top = jnp.max(both, axis=1, keepdims=True)
+        weights = jnp.exp(both - top)
+        total = jnp.sum(weights, axis=1, keepdims=True)
+        weights = weights.astype(bf16)
         image_sums = jnp.dot(
-            image_w.astype(bf16), block[:, side:], preferred_element_type=f32
+            weights[:, text_dev:], block[:, side:], preferred_element_type=f32
         )
         for d in range(1, seq_count):
             at = slice((d - 1) * PAD, d * PAD)
             text_sums = jnp.dot(
-                text_w[at].astype(bf16), text[l, :, lanes_of(d, kvw)],
+                weights[at, :text_dev], text[l, :, lanes_of(d, kvw)],
                 preferred_element_type=f32,
             )
             part_out[l, d, :, :HEAD_DIM] = (
@@ -428,28 +436,38 @@
 
     settle(keys_in.at[others], own_recv.at[0])
     own_keys = [keys_in[:, l].reshape(src_rows, HEAD_DIM) for l in range(layers)]
+    own_scores = jnp.concatenate(
+        [
+            jnp.concatenate(
+                [
+                    scores[l, :PAD, :],
+                    lax.dot_general(
+                        head_block(l, 0).astype(bf16), own_keys[l], NT,
+                        preferred_element_type=f32,
+                    ) * scale,
+                ],
+                axis=1,
+            )
+            for l in range(layers)
+        ],
+        axis=0,
+    )
+    own_top = jnp.max(own_scores, axis=1, keepdims=True)
+    own_w = jnp.exp(own_scores - own_top)
+    own_total = jnp.sum(own_w, axis=1, keepdims=True)
+    rounded = own_w.astype(bf16)
+    weights_out[...] = rounded[:, text_dev:]
     mine_now = []
     for l in range(layers):
-        image_scores = lax.dot_general(
-            head_block(l, 0).astype(bf16), own_keys[l], NT, preferred_element_type=f32
-        ) * scale
-        text_scores = scores[l, :PAD, :]
-        top = jnp.maximum(
-            jnp.max(text_scores, axis=1, keepdims=True),
-            jnp.max(image_scores, axis=1, keepdims=True),
-        )
-        text_w = jnp.exp(text_scores - top)
-        image_w = jnp.exp(image_scores - top)
-        total = jnp.sum(text_w, axis=1, keepdims=True) + jnp.sum(
-            image_w, axis=1, keepdims=True
-        )
+        at = slice(l * PAD, (l + 1) * PAD)
         value = jnp.dot(
-            text_w.astype(bf16), text[l, :, lanes_of(0, kvw)], preferred_element_type=f32
-        )
-        weights_out[l * PAD:(l + 1) * PAD, :] = image_w
-        mine_now.append(
-            (value, jnp.broadcast_to(top, (PAD, HEAD_DIM)), jnp.broadcast_to(total, (PAD, HEAD_DIM)))
-        )
+            rounded[at, :text_dev], text[l, :, lanes_of(0, kvw)], preferred_element_type=f32
+        )
+        mine_now.append((
+            value,
+            jnp.broadcast_to(own_top[at], (PAD, HEAD_DIM)),
+            jnp.broadcast_to(own_total[at], (PAD, HEAD_DIM)),
+        ))
     moved = jnp.dot(
         put, jnp.concatenate(own_keys, axis=1), preferred_element_type=f32
     ).astype(bf16)
@@ -501,7 +519,7 @@
                 cache.at[l, 0, :, lanes_of(d)], cache_out.at[l, 0, :, lanes_of(d)], sem.at[0]
             ).start()
     own = [values[:, l].reshape(src_rows, HEAD_DIM) for l in range(layers)]
-    both = jnp.concatenate([put[...], weights[...].astype(bf16)], axis=0)
+    both = jnp.concatenate([put[...], weights[...]], axis=0)
     moved = jnp.dot(both, jnp.concatenate(own, axis=1), preferred_element_type=f32)
     for l in range(layers):
         at = slice(l * HEAD_DIM, (l + 1) * HEAD_DIM)
@@ -532,7 +550,7 @@
     src_rows = image_rows.shape[1]
     groups = patch_count * req_count
     assert req_dev == 1 and seq_count == KV_HEADS and full == 2 * KV_HEADS * HEAD_DIM
-    assert patch_count % 2 == 0
+    assert patch_count % 2 == 0 and layers > 2
     per = src_rows // groups
     main_width = full - 2 * HEAD_DIM
     rows_padded = KV_HEADS * PAD
@@ -550,7 +568,7 @@
             pltpu.VMEM(cache_shape.shape, bf16),
             pltpu.VMEM((src_rows, src_rows), bf16),
             pltpu.VMEM((groups, layers, per, HEAD_DIM), bf16),
-            pltpu.VMEM((layers * PAD, src_rows), f32),
+            pltpu.VMEM((layers * PAD, src_rows), bf16),
             pltpu.VMEM((layers, PAD, 3 * HEAD_DIM), f32),
         ),
         in_specs=[hbm, pl.BlockSpec(memory_space=pl.ANY), hbm, hbm, hbm, hbm],
@@ -572,8 +590,8 @@
             pltpu.VMEM((layers, rows_padded, text_dev), f32),
             pltpu.VMEM((layers, seq_count, PAD, 3 * HEAD_DIM), f32),
             pltpu.VMEM((layers, seq_count, PAD, 3 * HEAD_DIM), f32),
-            dma((4,)), dma((3,)), dma((1,)), dma((1,)), dma((layers,)), dma((1,)), dma((2,)),
-            dma((2,)), dma((2,)), pltpu.SemaphoreType.REGULAR((4,)),
+            dma((1,)), dma((4,)), dma((1,)), dma((layers,)), dma((1,)), dma((2,)),
+            dma((2,)), dma((2,)), pltpu.SemaphoreType.REGULAR((3,)),
         ],
         compiler_params=pltpu.CompilerParams(
             collective_id=0, has_side_effects=True, vmem_limit_bytes=32 * 1024 * 1024

time: 51.8 us -> 51.6 us (level)
  no operation moved by 1% of the time
where the time goes in v5:
time: 51.6 us; the launch traced here: 51.4 us
  Pallas kernels  50.1 us (97%)
  between operations  1.28 us (2%)
    pallas_call x1, Pallas kernels, body(): pl.pallas_call(functools.partial(exchange, dims), out_shape=(pltpu.VMEM(c...  48.7 us
    pallas_call x1, Pallas kernels, body(): pl.pallas_call(functools.partial(finish, dims), out_shape=(att_shape, cac...  1.33 us

profile of v5, /device:TPU:9, one launch (start us, length us, event | category | flops | bytes accessed | tf_op | source)
XLA Modules:
  0.0 51.4 jit_solution(3570472941837394400)
XLA Ops:
  1.3 48.7 %shard_map.77 = (bf16[4,1,256,1024]{3,2,1,0:T(8,128)(2,1)S(1)}, bf16[256,256]{1,0:T(8,128)(2,1)S(1)}, bf16[8,4,32,128]{3,2,1,0:T(8,128)(2,1)S(1)}, bf16[32,256]{1,0:T(8,128)(2,1)S(1)}, f32[4,8,384]{2,1,0:T(8,128)S(1)}) custom-call(bf16[4,3584]{1,0:T(4,128)(2,1)} %bitcast.4, s32[1]{0:T(128)S(6)} %copy.8.len_hbm, s32[1,256]{1,0:T(1,128)} %bitcast.5, ...), custom_call_target="tpu_custom_call" | custom-call | tf_op jit(solution)/shard_map/pallas_call | solution.py:565
  50.0 1.3 %shard_map.78 = (bf16[4,896]{1,0:T(4,128)(2,1)}, bf16[4,1,256,1024]{3,2,1,0:T(8,128)(2,1)}) custom-call(bf16[4,1,256,1024]{3,2,1,0:T(8,128)(2,1)S(1)} %get-tuple-element.9.cache, bf16[256,256]{1,0:T(8,128)(2,1)S(1)} %get-tuple-element.10.put, bf16[8,4,32,128]{3,2,1,0:T(8,128)(2,1)S(1)} %get-tuple-element.11.values, ...), custom_call_target="tpu_custom_call" | custom-call | tf_op jit(solution)/shard_map/pallas_call | solution.py:604

commit v6 on v5

--- a/solution.py
+++ b/solution.py
@@ -30,7 +30,7 @@
     query_hbm, len_hbm, map_hbm, place_hbm, rows_hbm, text_hbm,
     cache, put_out, values_in, weights_out, partial_out,
     query, length, maps, places, rows, text, main_out, main_in, own_out, keys_in, place_out, place_in,
-    heads, scores, part_out, part_in,
+    heads, scores, part_out, part_in, first_out,
     small_sem, load_sem, main_send, main_recv, own_send, own_recv, place_sem, part_sem,
     info,
 ):
@@ -66,15 +66,10 @@
 
     others = pl.ds(0, groups - 1)
     own_in = (keys_in, values_in)
-    halves = (pl.ds(0, kvw), pl.ds(kvw, kvw))
-    first_rows = [
-        pltpu.make_async_copy(rows_hbm.at[0, :, at], rows.at[0, :, at], load_sem.at[i])
-        for i, at in enumerate(halves)
-    ]
-    second_rows = pltpu.make_async_copy(rows_hbm.at[1], rows.at[1], load_sem.at[2])
+    second_rows = pltpu.make_async_copy(rows_hbm.at[1], rows.at[1], load_sem.at[0])
     rest = pl.ds(2, layers - 2)
-    rest_rows = pltpu.make_async_copy(rows_hbm.at[rest], rows.at[rest], load_sem.at[3])
-    text_copy = pltpu.make_async_copy(text_hbm.at[:, 0], text, load_sem.at[0])
+    rest_rows = pltpu.make_async_copy(rows_hbm.at[rest], rows.at[rest], load_sem.at[1])
+    text_copy = pltpu.make_async_copy(text_hbm.at[:, 0], text, load_sem.at[2])
 
     def settle(ref, sem):
         pltpu.make_async_copy(ref, ref, sem).wait()
@@ -85,9 +80,17 @@
         pltpu.make_async_copy(query_hbm, query, small_sem.at[0]),
         pltpu.make_async_copy(len_hbm, length, small_sem.at[0]),
     ]
+    def lanes_of(d, base=0):
+        g = lax.rem(seq + d, seq_count)
+        return pl.ds(pl.multiple_of(base + g * HEAD_DIM, HEAD_DIM), HEAD_DIM)
+
+    def load(i, at):
+        pltpu.make_async_copy(rows_hbm.at[0, :, at], rows.at[0, :, at], load_sem.at[i]).start()
+
     small[0].start()
-    for copy in first_rows:
-        copy.start()
+    load(0, lanes_of(1))
+    for d in range(2, seq_count):
+        load(1, lanes_of(d))
     barrier = pltpu.get_barrier_semaphore()
 
     def tell(sem, p, s, r):
@@ -113,6 +116,8 @@
         for d in range(1, seq_count):
             tell(barrier, patch, lax.rem(seq + d, seq_count), req)
 
+    for d in range(1, seq_count):
+        load(2, lanes_of(d, kvw))
     has_below = 1 - (patch_count - 1 - patch) // (patch_count - 1)
     arrivals = (
         req_count - 1 + req_count * (has_below + 1 - upper) + (seq_count - 1) * (1 - has_below)
@@ -124,23 +129,26 @@
         pl.semaphore_wait(barrier, arrivals)
         tell(info.at[0], patch - 1, seq, req)
 
-
-    def lanes_of(d, base=0):
-        g = lax.rem(seq + d, seq_count)
-        return pl.ds(pl.multiple_of(base + g * HEAD_DIM, HEAD_DIM), HEAD_DIM)
 
     owner = lax.broadcasted_iota(jnp.int32, (groups, src_rows), 0)
     row_i = lax.broadcasted_iota(jnp.int32, (src_rows, src_rows), 0)
     col_i = lax.broadcasted_iota(jnp.int32, (src_rows, src_rows), 1)
     before = (row_i < col_i).astype(f32).astype(bf16)
     small[0].wait()
+    load(3, lanes_of(0))
+    load(3, lanes_of(0, kvw))
     small[1].start()
     mine = maps[...] == owner
     rank = jnp.dot(mine.astype(f32).astype(bf16), before, preferred_element_type=f32)
     slot = jnp.sum(
         jnp.where(mine, rank + (owner * per).astype(f32), 0.0), axis=0, keepdims=True
     )
-    pick = (row_i == slot.astype(jnp.int32)).astype(f32).astype(bf16)
+    slot = slot.astype(jnp.int32)
+    p_first, _ = partner(far[-1][0])
+    row_first = lax.broadcasted_iota(jnp.int32, (req_count * per, src_rows), 0)
+    pick_first = (
+        row_first + p_first * (req_count * per) == slot
+    ).astype(f32).astype(bf16)
 
     def place_copy(hop):
         p, r = partner(hop)
@@ -158,6 +166,14 @@
             device_id=(p, seq, r), device_id_type=MESH,
         )
 
+    def first_copy(hop):
+        p, r = partner(hop)
+        return pltpu.make_async_remote_copy(
+            src_ref=first_out.at[r], dst_ref=main_in.at[0, me, :, pl.ds(0, HEAD_DIM)],
+            send_sem=main_send.at[0], recv_sem=main_recv.at[0],
+            device_id=(p, seq, r), device_id_type=MESH,
+        )
+
     def own_copy(i, hop):
         p, r = partner(hop)
         return pltpu.make_async_remote_copy(
@@ -182,7 +198,7 @@
         at = slice(0, side) if base == 0 else slice(side, main_width)
         main_out[l, :, :, at] = moved.reshape(groups, per, side)
 
-    def send_first(l, at):
+    def send_first(l, at, across):
         for hop in mates:
             main_copy(l, hop, at).start()
 
@@ -196,23 +212,35 @@
             @pl.when(inner)
             def _():
                 for hop in far[-1]:
-                    main_copy(l, hop, at).start()
-
+                    main_copy(l, hop, across).start()
+
+    def settle_rows(i, width):
+        settle(rows.at[0, :, pl.ds(0, width)], load_sem.at[i])
+
+    settle_rows(0, HEAD_DIM)
+    second_rows.start()
+    moved = jnp.dot(pick_first, rows[0, :, lanes_of(1)], preferred_element_type=f32)
+    first_out[...] = moved.astype(bf16).reshape(req_count, per, HEAD_DIM)
+
+    @pl.when(jnp.logical_not(answers))
+    def _():
+        pl.semaphore_wait(barrier, arrivals)
+
+    @pl.when(inner)
+    def _():
+        for hop in far[-1]:
+            first_copy(hop).start()
+
+    pick = (row_i == slot).astype(f32).astype(bf16)
     for l in range(layers):
         if l == 0:
-            first_rows[0].wait()
-            second_rows.start()
+            settle_rows(1, side - HEAD_DIM)
             rest_rows.start()
             sort(l, 0)
-
-            @pl.when(jnp.logical_not(answers))
-            def _():
-                pl.semaphore_wait(barrier, arrivals)
-
-            send_first(l, pl.ds(0, side))
-            first_rows[1].wait()
+            send_first(l, pl.ds(0, side), pl.ds(HEAD_DIM, side - HEAD_DIM))
+            settle_rows(2, side)
             sort(l, kvw)
-            send_first(l, pl.ds(side, side))
+            send_first(l, pl.ds(side, side), pl.ds(side, side))
 
             @pl.when(jnp.logical_and(patch == 1, above))
             def _():
@@ -225,7 +253,7 @@
                 rest_rows.wait()
             sort(l, 0)
             sort(l, kvw)
-            send_first(l, pl.ds(0, main_width))
+            send_first(l, pl.ds(0, main_width), pl.ds(0, main_width))
         if l == 0:
             small[1].wait()
             small[2].start()
@@ -244,6 +272,7 @@
                 for hop in beside:
                     place_copy(hop).start()
 
+    settle_rows(3, 2 * HEAD_DIM)
     for l in range(layers):
         turned = jnp.concatenate([rows[l, :, lanes_of(0)], rows[l, :, lanes_of(0, kvw)]], axis=1)
         moved = jnp.dot(pick, turned, preferred_element_type=f32).astype(bf16)
@@ -510,23 +539,20 @@
         g = lax.rem(seq + d, seq_count)
         return pl.ds(pl.multiple_of(kvw + g * HEAD_DIM, HEAD_DIM), HEAD_DIM)
 
-    for l in range(layers):
-        pltpu.make_async_copy(
-            cache.at[l, 0, :, pl.ds(0, kvw)], cache_out.at[l, 0, :, pl.ds(0, kvw)], sem.at[0]
-        ).start()
-        for d in range(1, seq_count):
-            pltpu.make_async_copy(
-                cache.at[l, 0, :, lanes_of(d)], cache_out.at[l, 0, :, lanes_of(d)], sem.at[0]
-            ).start()
+    def write(piece, at):
+        pltpu.make_async_copy(piece, cache_out.at[:, 0, :, at], sem.at[0]).start()
+
+    keys = pl.ds(0, kvw)
+    write(cache.at[:, 0, :, keys], keys)
+    for d in range(1, seq_count):
+        write(cache.at[:, 0, :, lanes_of(d)], lanes_of(d))
     own = [values[:, l].reshape(src_rows, HEAD_DIM) for l in range(layers)]
     both = jnp.concatenate([put[...], weights[...]], axis=0)
     moved = jnp.dot(both, jnp.concatenate(own, axis=1), preferred_element_type=f32)
     for l in range(layers):
         at = slice(l * HEAD_DIM, (l + 1) * HEAD_DIM)
         last[l] = moved[:src_rows, at].astype(bf16)
-        pltpu.make_async_copy(
-            last.at[l], cache_out.at[l, 0, :, lanes_of(0)], sem.at[0]
-        ).start()
+    write(last, lanes_of(0))
     lines = []
     for l in range(layers):
         value = moved[
@@ -590,6 +616,7 @@
             pltpu.VMEM((layers, rows_padded, text_dev), f32),
             pltpu.VMEM((layers, seq_count, PAD, 3 * HEAD_DIM), f32),
             pltpu.VMEM((layers, seq_count, PAD, 3 * HEAD_DIM), f32),
+            pltpu.VMEM((req_count, per, HEAD_DIM), bf16),
             dma((1,)), dma((4,)), dma((1,)), dma((layers,)), dma((1,)), dma((2,)),
             dma((2,)), dma((2,)), pltpu.SemaphoreType.REGULAR((3,)),
         ],

time: 51.6 us -> 51.6 us (level)
  no operation moved by 1% of the time
where the time goes in v6:
time: 51.6 us; the launch traced here: 51.3 us
  Pallas kernels  50 us (97%)
  between operations  1.28 us (2%)
    pallas_call x1, Pallas kernels, body(): pl.pallas_call(functools.partial(exchange, dims), out_shape=(pltpu.VMEM(c...  48.6 us
    pallas_call x1, Pallas kernels, body(): pl.pallas_call(functools.partial(finish, dims), out_shape=(att_shape, cac...  1.34 us

profile of v6, /device:TPU:9, one launch (start us, length us, event | category | flops | bytes accessed | tf_op | source)
XLA Modules:
  0.0 51.3 jit_solution(4985411460983968253)
XLA Ops:
  1.3 48.6 %shard_map.77 = (bf16[4,1,256,1024]{3,2,1,0:T(8,128)(2,1)S(1)}, bf16[256,256]{1,0:T(8,128)(2,1)S(1)}, bf16[8,4,32,128]{3,2,1,0:T(8,128)(2,1)S(1)}, bf16[32,256]{1,0:T(8,128)(2,1)S(1)}, f32[4,8,384]{2,1,0:T(8,128)S(1)}) custom-call(bf16[4,3584]{1,0:T(4,128)(2,1)} %bitcast.4, s32[1]{0:T(128)S(6)} %copy.8.len_hbm, s32[1,256]{1,0:T(1,128)} %bitcast.5, ...), custom_call_target="tpu_custom_call" | custom-call | tf_op jit(solution)/shard_map/pallas_call | solution.py:591
  49.9 1.3 %shard_map.78 = (bf16[4,896]{1,0:T(4,128)(2,1)}, bf16[4,1,256,1024]{3,2,1,0:T(8,128)(2,1)}) custom-call(bf16[4,1,256,1024]{3,2,1,0:T(8,128)(2,1)S(1)} %get-tuple-element.9.cache, bf16[256,256]{1,0:T(8,128)(2,1)S(1)} %get-tuple-element.10.put, bf16[8,4,32,128]{3,2,1,0:T(8,128)(2,1)S(1)} %get-tuple-element.11.values, ...), custom_call_target="tpu_custom_call" | custom-call | tf_op jit(solution)/shard_map/pallas_call | solution.py:631

commit v7 on v6

--- a/solution.py
+++ b/solution.py
@@ -31,7 +31,7 @@
     cache, put_out, values_in, weights_out, partial_out,
     query, length, maps, places, rows, text, main_out, main_in, own_out, keys_in, place_out, place_in,
     heads, scores, part_out, part_in, first_out,
-    small_sem, load_sem, main_send, main_recv, own_send, own_recv, place_sem, part_sem,
+    small_sem, load_sem, send_sem, main_recv, own_recv, late_recv,
     info,
 ):
     patch_count, seq_count, req_count = dims
@@ -89,33 +89,33 @@
 
     small[0].start()
     load(0, lanes_of(1))
+    barrier = pltpu.get_barrier_semaphore()
+
+    def tell(sem, p, s, r):
+        pl.semaphore_signal(sem, inc=1, device_id=(p, s, r), device_id_type=MESH)
+
+    above, below = patch < patch_count - 1, patch > 0
+
+    @pl.when(jnp.logical_and(below, patch <= half))
+    def _():
+        for c in range(req_count):
+            tell(barrier, patch - 1, seq, lax.rem(req + c, req_count))
+
+    @pl.when(above)
+    def _():
+        for c in range(req_count):
+            tell(barrier, patch + 1, seq, lax.rem(req + c, req_count))
+
+    for c in range(1, req_count):
+        tell(barrier, patch, seq, lax.rem(req + c, req_count))
+
+    @pl.when(patch == 0)
+    def _():
+        for d in range(1, seq_count):
+            tell(barrier, patch, lax.rem(seq + d, seq_count), req)
+
     for d in range(2, seq_count):
         load(1, lanes_of(d))
-    barrier = pltpu.get_barrier_semaphore()
-
-    def tell(sem, p, s, r):
-        pl.semaphore_signal(sem, inc=1, device_id=(p, s, r), device_id_type=MESH)
-
-    above, below = patch < patch_count - 1, patch > 0
-
-    @pl.when(jnp.logical_and(below, patch <= half))
-    def _():
-        for c in range(req_count):
-            tell(barrier, patch - 1, seq, lax.rem(req + c, req_count))
-
-    @pl.when(above)
-    def _():
-        for c in range(req_count):
-            tell(barrier, patch + 1, seq, lax.rem(req + c, req_count))
-
-    for c in range(1, req_count):
-        tell(barrier, patch, seq, lax.rem(req + c, req_count))
-
-    @pl.when(patch == 0)
-    def _():
-        for d in range(1, seq_count):
-            tell(barrier, patch, lax.rem(seq + d, seq_count), req)
-
     for d in range(1, seq_count):
         load(2, lanes_of(d, kvw))
     has_below = 1 - (patch_count - 1 - patch) // (patch_count - 1)
@@ -131,12 +131,11 @@
 
 
     owner = lax.broadcasted_iota(jnp.int32, (groups, src_rows), 0)
+    source = lax.broadcasted_iota(jnp.int32, (groups, src_rows), 1) // per
     row_i = lax.broadcasted_iota(jnp.int32, (src_rows, src_rows), 0)
     col_i = lax.broadcasted_iota(jnp.int32, (src_rows, src_rows), 1)
     before = (row_i < col_i).astype(f32).astype(bf16)
     small[0].wait()
-    load(3, lanes_of(0))
-    load(3, lanes_of(0, kvw))
     small[1].start()
     mine = maps[...] == owner
     rank = jnp.dot(mine.astype(f32).astype(bf16), before, preferred_element_type=f32)
@@ -153,8 +152,8 @@
     def place_copy(hop):
         p, r = partner(hop)
         return pltpu.make_async_remote_copy(
-            src_ref=place_out, dst_ref=place_in.at[me],
-            send_sem=place_sem.at[0], recv_sem=place_sem.at[1],
+            src_ref=place_out.at[p * req_count + r], dst_ref=place_in.at[me],
+            send_sem=send_sem.at[1], recv_sem=late_recv.at[0],
             device_id=(p, seq, r), device_id_type=MESH,
         )
 
@@ -162,7 +161,7 @@
         p, r = partner(hop)
         return pltpu.make_async_remote_copy(
             src_ref=main_out.at[l, p * req_count + r, :, at], dst_ref=main_in.at[l, me, :, at],
-            send_sem=main_send.at[0], recv_sem=main_recv.at[l],
+            send_sem=send_sem.at[0], recv_sem=main_recv.at[l],
             device_id=(p, seq, r), device_id_type=MESH,
         )
 
@@ -170,7 +169,7 @@
         p, r = partner(hop)
         return pltpu.make_async_remote_copy(
             src_ref=first_out.at[r], dst_ref=main_in.at[0, me, :, pl.ds(0, HEAD_DIM)],
-            send_sem=main_send.at[0], recv_sem=main_recv.at[0],
+            send_sem=send_sem.at[0], recv_sem=main_recv.at[0],
             device_id=(p, seq, r), device_id_type=MESH,
         )
 
@@ -178,7 +177,7 @@
         p, r = partner(hop)
         return pltpu.make_async_remote_copy(
             src_ref=own_out.at[i, p * req_count + r], dst_ref=own_in[i].at[me],
-            send_sem=own_send.at[0], recv_sem=own_recv.at[i],
+            send_sem=send_sem.at[2], recv_sem=own_recv.at[i],
             device_id=(p, seq, r), device_id_type=MESH,
         )
 
@@ -186,7 +185,7 @@
         s = lax.rem(seq + d, seq_count)
         return pltpu.make_async_remote_copy(
             src_ref=part_out.at[l, d], dst_ref=part_in.at[l, d],
-            send_sem=part_sem.at[0], recv_sem=part_sem.at[1],
+            send_sem=send_sem.at[1], recv_sem=late_recv.at[1],
             device_id=(patch, s, req), device_id_type=MESH,
         )
 
@@ -239,6 +238,8 @@
             sort(l, 0)
             send_first(l, pl.ds(0, side), pl.ds(HEAD_DIM, side - HEAD_DIM))
             settle_rows(2, side)
+            load(2, lanes_of(0))
+            load(2, lanes_of(0, kvw))
             sort(l, kvw)
             send_first(l, pl.ds(side, side), pl.ds(side, side))
 
@@ -262,8 +263,13 @@
                 jnp.broadcast_to(local, (PAD, src_rows)), pick, NT,
                 preferred_element_type=f32,
             )
-            place_out[...] = place_sorted[0:1].astype(jnp.int32)
-            place_in[me] = place_sorted[0:1].astype(jnp.int32)
+            apart = jnp.where(source == owner, place_sorted[0:1], 0.0).astype(bf16)
+            lane = lax.broadcasted_iota(jnp.int32, (src_rows, HEAD_DIM), 1)
+            entry = lax.broadcasted_iota(jnp.int32, (src_rows, HEAD_DIM), 0)
+            gather = (lax.rem(entry, per) == lane).astype(f32).astype(bf16)
+            placed = jnp.dot(apart, gather, preferred_element_type=f32).astype(jnp.int32)
+            place_out[...] = placed.reshape(groups, 1, HEAD_DIM)
+            place_in[me] = place_out[me]
             for hop in mates:
                 place_copy(hop).start()
 
@@ -272,7 +278,7 @@
                 for hop in beside:
                     place_copy(hop).start()
 
-    settle_rows(3, 2 * HEAD_DIM)
+    settle_rows(2, 2 * HEAD_DIM)
     for l in range(layers):
         turned = jnp.concatenate([rows[l, :, lanes_of(0)], rows[l, :, lanes_of(0, kvw)]], axis=1)
         moved = jnp.dot(pick, turned, preferred_element_type=f32).astype(bf16)
@@ -406,13 +412,14 @@
     def _():
         pl.semaphore_wait(info.at[2], 1)
 
-    settle(place_in.at[others], place_sem.at[1])
-    wanted = (row_i == me * per + lax.rem(col_i, per)).astype(f32).astype(bf16)
+    settle(place_in.at[others], late_recv.at[0])
+    slot_i = lax.broadcasted_iota(jnp.int32, (HEAD_DIM, src_rows), 0)
+    place_i = lax.broadcasted_iota(jnp.int32, (HEAD_DIM, src_rows), 1)
+    wanted = (slot_i == lax.rem(place_i, per)).astype(f32).astype(bf16)
     lanes = jnp.dot(
-        place_in[...].reshape(groups, src_rows).astype(f32).astype(bf16), wanted,
+        place_in[...].reshape(groups, HEAD_DIM).astype(f32).astype(bf16), wanted,
         preferred_element_type=f32,
     )
-    source = lax.broadcasted_iota(jnp.int32, (groups, src_rows), 1) // per
     place = jnp.sum(jnp.where(source == owner, lanes, 0.0), axis=0, keepdims=True)
     put = (row_i == place.astype(jnp.int32)).astype(f32).astype(bf16)
     put_out[...] = put
@@ -430,6 +437,8 @@
             axis=0,
         ).astype(bf16)
         settle(main_in.at[l, others], main_recv.at[l])
+        if l == 0:
+            settle(place_in.at[others], send_sem.at[1])
         block = main_in[l].reshape(src_rows, main_width)
         image_scores = lax.dot_general(
             spread, block[:, :side], NT, preferred_element_type=f32
@@ -504,7 +513,7 @@
         cache[l, 0, :, lanes_of(0)] = moved[:, l * HEAD_DIM:(l + 1) * HEAD_DIM]
 
     bands = pl.ds(1, seq_count - 1)
-    settle(part_in.at[:, bands], part_sem.at[1])
+    settle(part_in.at[:, bands], late_recv.at[1])
     for l in range(layers):
         cells = [mine_now[l]] + [
             tuple(part_in[l, d, :, i * HEAD_DIM:(i + 1) * HEAD_DIM] for i in range(3))
@@ -518,10 +527,9 @@
         )
         partial_out[l, :, 2 * HEAD_DIM:] = sum(f * c[2] for f, c in zip(factors, cells))
 
-    settle(main_out.at[:, others], main_send.at[0])
-    settle(place_in.at[others], place_sem.at[0])
-    settle(part_out.at[:, bands], part_sem.at[0])
-    settle(own_out.at[:, others], own_send.at[0])
+    settle(part_out.at[:, bands], send_sem.at[1])
+    settle(main_out.at[:, others], send_sem.at[0])
+    settle(own_out.at[:, others], send_sem.at[2])
     settle(values_in.at[others], own_recv.at[1])
 
 
@@ -576,8 +584,8 @@
     src_rows = image_rows.shape[1]
     groups = patch_count * req_count
     assert req_dev == 1 and seq_count == KV_HEADS and full == 2 * KV_HEADS * HEAD_DIM
-    assert patch_count % 2 == 0 and layers > 2
     per = src_rows // groups
+    assert patch_count % 2 == 0 and layers > 2 and per <= HEAD_DIM
     main_width = full - 2 * HEAD_DIM
     rows_padded = KV_HEADS * PAD
     bf16, f32, i32 = jnp.bfloat16, jnp.float32, jnp.int32
@@ -610,15 +618,14 @@
             pltpu.VMEM((layers, groups, per, main_width), bf16),
             pltpu.VMEM((2, groups, layers, per, HEAD_DIM), bf16),
             pltpu.VMEM((groups, layers, per, HEAD_DIM), bf16),
-            pltpu.VMEM((1, src_rows), i32),
-            pltpu.VMEM((groups, 1, src_rows), i32),
+            pltpu.VMEM((groups, 1, HEAD_DIM), i32),
+            pltpu.VMEM((groups, 1, HEAD_DIM), i32),
             pltpu.VMEM((layers, rows_padded, HEAD_DIM), f32),
             pltpu.VMEM((layers, rows_padded, text_dev), f32),
             pltpu.VMEM((layers, seq_count, PAD, 3 * HEAD_DIM), f32),
             pltpu.VMEM((layers, seq_count, PAD, 3 * HEAD_DIM), f32),
             pltpu.VMEM((req_count, per, HEAD_DIM), bf16),
-            dma((1,)), dma((4,)), dma((1,)), dma((layers,)), dma((1,)), dma((2,)),
-            dma((2,)), dma((2,)), pltpu.SemaphoreType.REGULAR((3,)),
+            dma((1,)), dma((3,)), dma((3,)), dma((layers,)), dma((2,)), dma((2,)), pltpu.SemaphoreType.REGULAR((3,)),
         ],
         compiler_params=pltpu.CompilerParams(
             collective_id=0, has_side_effects=True, vmem_limit_bytes=32 * 1024 * 1024

time: 51.6 us -> 51.5 us (level)
  no operation moved by 1% of the time
where the time goes in v7:
time: 51.5 us; the launch traced here: 51.2 us
  Pallas kernels  49.9 us (97%)
  between operations  1.28 us (2%)
    pallas_call x1, Pallas kernels, body(): pl.pallas_call(functools.partial(exchange, dims), out_shape=(pltpu.VMEM(c...  48.5 us
    pallas_call x1, Pallas kernels, body(): pl.pallas_call(functools.partial(finish, dims), out_shape=(att_shape, cac...  1.34 us

profile of v7, /device:TPU:9, one launch (start us, length us, event | category | flops | bytes accessed | tf_op | source)
XLA Modules:
  0.0 51.2 jit_solution(16953213987283160408)
XLA Ops:
  1.3 48.5 %shard_map.77 = (bf16[4,1,256,1024]{3,2,1,0:T(8,128)(2,1)S(1)}, bf16[256,256]{1,0:T(8,128)(2,1)S(1)}, bf16[8,4,32,128]{3,2,1,0:T(8,128)(2,1)S(1)}, bf16[32,256]{1,0:T(8,128)(2,1)S(1)}, f32[4,8,384]{2,1,0:T(8,128)S(1)}) custom-call(bf16[4,3584]{1,0:T(4,128)(2,1)} %bitcast.4, s32[1]{0:T(128)S(6)} %copy.8.len_hbm, s32[1,256]{1,0:T(1,128)} %bitcast.5, ...), custom_call_target="tpu_custom_call" | custom-call | tf_op jit(solution)/shard_map/pallas_call | solution.py:599
  49.8 1.3 %shard_map.78 = (bf16[4,896]{1,0:T(4,128)(2,1)}, bf16[4,1,256,1024]{3,2,1,0:T(8,128)(2,1)}) custom-call(bf16[4,1,256,1024]{3,2,1,0:T(8,128)(2,1)S(1)} %get-tuple-element.9.cache, bf16[256,256]{1,0:T(8,128)(2,1)S(1)} %get-tuple-element.10.put, bf16[8,4,32,128]{3,2,1,0:T(8,128)(2,1)S(1)} %get-tuple-element.11.values, ...), custom_call_target="tpu_custom_call" | custom-call | tf_op jit(solution)/shard_map/pallas_call | solution.py:638

commit v8 on v7

--- a/solution.py
+++ b/solution.py
@@ -547,20 +547,22 @@
         g = lax.rem(seq + d, seq_count)
         return pl.ds(pl.multiple_of(kvw + g * HEAD_DIM, HEAD_DIM), HEAD_DIM)
 
-    def write(piece, at):
-        pltpu.make_async_copy(piece, cache_out.at[:, 0, :, at], sem.at[0]).start()
-
-    keys = pl.ds(0, kvw)
-    write(cache.at[:, 0, :, keys], keys)
-    for d in range(1, seq_count):
-        write(cache.at[:, 0, :, lanes_of(d)], lanes_of(d))
+    def write(l, piece, at):
+        pltpu.make_async_copy(piece, cache_out.at[l, 0, :, at], sem.at[0]).start()
+
+    for l in range(layers):
+        for g in range(seq_count):
+            keys = pl.ds(g * HEAD_DIM, HEAD_DIM)
+            write(l, cache.at[l, 0, :, keys], keys)
+        for d in range(1, seq_count):
+            write(l, cache.at[l, 0, :, lanes_of(d)], lanes_of(d))
     own = [values[:, l].reshape(src_rows, HEAD_DIM) for l in range(layers)]
     both = jnp.concatenate([put[...], weights[...]], axis=0)
     moved = jnp.dot(both, jnp.concatenate(own, axis=1), preferred_element_type=f32)
     for l in range(layers):
         at = slice(l * HEAD_DIM, (l + 1) * HEAD_DIM)
         last[l] = moved[:src_rows, at].astype(bf16)
-    write(last, lanes_of(0))
+        write(l, last.at[l], lanes_of(0))
     lines = []
     for l in range(layers):
         value = moved[

time: 51.5 us -> 51.5 us (level)
  no operation moved by 1% of the time
where the time goes in v8:
time: 51.5 us; the launch traced here: 51.2 us
  Pallas kernels  49.9 us (97%)
  between operations  1.28 us (2%)
    pallas_call x1, Pallas kernels, body(): pl.pallas_call(functools.partial(exchange, dims), out_shape=(pltpu.VMEM(c...  48.5 us
    pallas_call x1, Pallas kernels, body(): pl.pallas_call(functools.partial(finish, dims), out_shape=(att_shape, cac...  1.32 us

profile of v8, /device:TPU:9, one launch (start us, length us, event | category | flops | bytes accessed | tf_op | source)
XLA Modules:
  0.0 51.2 jit_solution(8182361851266473734)
XLA Ops:
  1.3 48.5 %shard_map.77 = (bf16[4,1,256,1024]{3,2,1,0:T(8,128)(2,1)S(1)}, bf16[256,256]{1,0:T(8,128)(2,1)S(1)}, bf16[8,4,32,128]{3,2,1,0:T(8,128)(2,1)S(1)}, bf16[32,256]{1,0:T(8,128)(2,1)S(1)}, f32[4,8,384]{2,1,0:T(8,128)S(1)}) custom-call(bf16[4,3584]{1,0:T(4,128)(2,1)} %bitcast.4, s32[1]{0:T(128)S(6)} %copy.8.len_hbm, s32[1,256]{1,0:T(1,128)} %bitcast.5, ...), custom_call_target="tpu_custom_call" | custom-call | tf_op jit(solution)/shard_map/pallas_call | solution.py:601
  49.8 1.3 %shard_map.78 = (bf16[4,896]{1,0:T(4,128)(2,1)}, bf16[4,1,256,1024]{3,2,1,0:T(8,128)(2,1)}) custom-call(bf16[4,1,256,1024]{3,2,1,0:T(8,128)(2,1)S(1)} %get-tuple-element.9.cache, bf16[256,256]{1,0:T(8,128)(2,1)S(1)} %get-tuple-element.10.put, bf16[8,4,32,128]{3,2,1,0:T(8,128)(2,1)S(1)} %get-tuple-element.11.values, ...), custom_call_target="tpu_custom_call" | custom-call | tf_op jit(solution)/shard_map/pallas_call | solution.py:640
